TPU v7x, 32 devices: a whole 2x2x4 slice. The times are simulated.
32 devices in a mesh: gx: 4 (over y, x), gy: 8 (over z, core).
Axes of the slice: x: 2, y: 2, z: 4, core: 2. Of those that a mesh axis runs over, the one named last changes fastest.
Arguments:
- schur_blocks: float32 [32, 2048, 2048], P(('gx', 'gy')), may hold values from -1 to 11, as said below
- offsets: int32 [32], P(('gx', 'gy')), may hold values from 256 to 768, as said below
- right_side: float32 [32768, 128], P(('gx', 'gy')), may hold values from -20 to 20
- coarse_basis: float32 [32768, 128], P(('gx', 'gy')), may hold values from -0.03125 to 0.03125
- coarse_load: float32 [128, 128], replicated, may hold values from -6 to 6
Outputs:
- multipliers: float32 [32768, 128], P(('gx', 'gy'))
- amplitudes: float32 [128, 128], replicated
Inputs may be any that keep to these rules, and one draw needn't show every extreme that they name: `schur_blocks`: each block is symmetric positive definite. `offsets`: both ends of the range are taken by some subdomain.
All inputs are finite; a program needn't handle non-finite values.
Results may differ from a plain program's by a relative error of at most 0.0003.
Values sent between devices are 32-bit elements; how exact they have to be, the bound alone decides.
No kernel may reach another device: no remote copies, remote signals or barrier semaphores. Data moves between devices by JAX's collectives and lax.ppermute only.
A program may use at most 128 MiB of HBM per device.

v0:
```python
import jax
import jax.numpy as jnp
from jax import lax
from jax.sharding import PartitionSpec as P

ITERS = 3


HIGHEST = lax.Precision.HIGHEST


def extended_2(block, sides, width):
    for axis, dim in sides:
        count = lax.axis_size(axis)
        forward = [(i, i + 1) for i in range(count - 1)]
        backward = [(target, source) for source, target in forward]
        low = lax.ppermute(
            lax.slice_in_dim(block, block.shape[dim] - width, None, axis=dim), axis, forward
        )
        high = lax.ppermute(lax.slice_in_dim(block, 0, width, axis=dim), axis, backward)
        block = jnp.concatenate([low, block, high], axis=dim)
    return block


def from_behind(value, axis, steps):
    count = lax.axis_size(axis)
    initial, last = (max(0, -steps), min(count, count - steps))
    return lax.ppermute(value, axis, [(source, source + steps) for source in range(initial, last)])


def apply_local(vector, schur_block, start_row):
    slab_rows = vector.shape[0]
    window_rows = schur_block.shape[0]
    extended = extended_2(vector, ((("gx", "gy"), 0),), slab_rows)
    window = lax.dynamic_slice_in_dim(extended, start_row, window_rows, 0)
    product_block = jnp.dot(
        schur_block, window, precision=HIGHEST, preferred_element_type=jnp.float32
    )
    spread = jnp.zeros((3 * slab_rows, vector.shape[1]), jnp.float32)
    spread = lax.dynamic_update_slice_in_dim(spread, product_block, start_row, 0)
    to_left = spread[:slab_rows]
    own_part = spread[slab_rows : 2 * slab_rows]
    to_right = spread[2 * slab_rows :]
    from_right = from_behind(to_left, ("gx", "gy"), -1)
    from_left = from_behind(to_right, ("gx", "gy"), 1)
    result = own_part + from_left + from_right
    return result


def project_sum(residual, coarse_basis, gram_factor):
    local_coarse = jnp.dot(
        coarse_basis.T, residual, precision=HIGHEST, preferred_element_type=jnp.float32
    )
    coarse_part, squares = lax.psum(
        (local_coarse, jnp.sum(residual * residual, axis=0)), ("gx", "gy")
    )
    amplitudes = jax.scipy.linalg.cho_solve((gram_factor, True), coarse_part)
    projected = residual - jnp.dot(
        coarse_basis, amplitudes, precision=HIGHEST, preferred_element_type=jnp.float32
    )
    energy = squares - jnp.sum(amplitudes * coarse_part, axis=0)
    return (projected, amplitudes, energy)


def local(schur_blocks, offsets, right_side, coarse_basis, coarse_load):
    schur_block = schur_blocks[0]
    start_row = offsets[0]
    local_gram = jnp.dot(
        coarse_basis.T, coarse_basis, precision=HIGHEST, preferred_element_type=jnp.float32
    )
    gram_matrix = lax.psum(local_gram, ("gx", "gy"))
    gram_factor = jnp.linalg.cholesky(gram_matrix)
    start_load = jax.scipy.linalg.cho_solve((gram_factor, True), coarse_load)
    multipliers = jnp.dot(
        coarse_basis, start_load, precision=HIGHEST, preferred_element_type=jnp.float32
    )
    residual = right_side - apply_local(multipliers, schur_block, start_row)
    projected, amplitudes, energy_now = project_sum(residual, coarse_basis, gram_factor)
    direction = projected
    for iteration in range(ITERS):
        operator_image = apply_local(direction, schur_block, start_row)
        curvature = lax.psum(jnp.sum(direction * operator_image, axis=0), ("gx", "gy"))
        step_length = energy_now / curvature
        multipliers = multipliers + step_length * direction
        residual = residual - step_length * operator_image
        projected, amplitudes, energy_next = project_sum(residual, coarse_basis, gram_factor)
        direction = projected + energy_next / energy_now * direction
        energy_now = energy_next
    return (multipliers, amplitudes)


def solution(mesh):
    in_specs = (
        P(("gx", "gy"), None, None),
        P(("gx", "gy")),
        P(("gx", "gy"), None),
        P(("gx", "gy"), None),
        P(),
    )
    out_specs = (P(("gx", "gy"), None), P())
    return jax.shard_map(local, mesh=mesh, in_specs=in_specs, out_specs=out_specs, check_vma=False)
```

profile of v0, /device:TPU:0, one launch (start us, length us, event | category | flops | bytes accessed | tf_op | source)
XLA Modules:
  0.0 1051.2 jit_solution(16787756393830020999)
XLA Ops:
  9.9 126.4 %all-reduce.7.cloned.1.call-done = f32[128,128]{0,1:T(8,128)} async-done(((f32[128,128]{0,1:T(8,128)}), f32[128,128]{0,1:T(8,128)}) %all-reduce.7.cloned.1.call-update) | async-done | bytes 65552 | tf_op jit(solution)/shard_map/psum | solution.py:71
  138.1 11.7 %cholesky.18 = f32[128,128]{1,0:T(8,128)S(1)} custom-call(f32[128,128]{1,0:T(8,128)S(1)} %fusion.66), custom_call_target="Cholesky" | custom-call | tf_op jit(solution)/shard_map/jit(cholesky)/cholesky | solution.py:72
  151.1 9.8 custom-call.12
  162.1 3.7 collective-permute-start
  170.3 20.9 %fusion.8 = f32[2048,128]{0,1:T(8,128)} fusion(f32[1,2048,2048]{2,1,0:T(8,128)} %param.7, s32[]{:T(128)S(6)} %select_n.7, f32[1024,128]{0,1:T(8,128)S(1)} %collective-permute-done, f32[1024,128]{0,1:T(8,128)S(1)} %convolution_bitcast_fusion.3, f32[1024,128]{0,1:T(8,128)S(1)} %collective-permute-done.1), kind=kOutput, calls=%fused_computation.8 | convolution fusion | flops 6442975232 | bytes 19398660 | tf_op jit(solution)/shard_map/dot_general | solution.py:36
  191.4 4.6 dynamic_update_slice.12
  198.3 14.7 %collective-permute-start.2 = (f32[1024,128]{0,1:T(8,128)}, f32[1024,128]{0,1:T(8,128)}, u32[]{:S(2)}, u32[]{:S(2)}) collective-permute-start(f32[1024,128]{0,1:T(8,128)} %get-tuple-element.25), channel_id=1, source_target_pairs={{0,1},{1,2},{2,3},{3,4},{4,5},{5,6},{6,7},{7,8},{8,9},{9,10},{10,1... | collective-permute-start | bytes 1572872 | tf_op jit(solution)/shard_map/ppermute | solution.py:28
  216.8 132.7 %all-reduce.9.cloned.1.call-done = f32[128,128]{0,1:T(8,128)} async-done(((f32[128,128]{0,1:T(8,128)}), f32[128,128]{0,1:T(8,128)}) %all-reduce.9.cloned.1.call-update) | async-done | bytes 65552 | tf_op jit(solution)/shard_map/psum | solution.py:54
  351.5 3.7 collective-permute-start.4
  356.7 3.1 collective-permute-done.5
  359.7 20.9 %fusion.11 = f32[2048,128]{0,1:T(8,128)} fusion(f32[1,2048,2048]{2,1,0:T(8,128)} %param.7, s32[]{:T(128)S(6)} %select_n.7, f32[1024,128]{0,1:T(8,128)S(1)} %collective-permute-done.4, f32[1024,128]{0,1:T(8,128)S(1)} %fusion.20, f32[1024,128]{0,1:T(8,128)S(1)} %collective-permute-done.5), kind=kOutput, calls=%fused_computation.9 | convolution fusion | flops 6442975232 | bytes 19398660 | tf_op jit(solution)/shard_map/dot_general | solution.py:36
  380.8 4.6 dynamic_update_slice.13
  387.7 14.7 %collective-permute-start.6 = (f32[1024,128]{0,1:T(8,128)}, f32[1024,128]{0,1:T(8,128)}, u32[]{:S(2)}, u32[]{:S(2)}) collective-permute-start(f32[1024,128]{0,1:T(8,128)} %get-tuple-element.23), channel_id=1, source_target_pairs={{0,1},{1,2},{2,3},{3,4},{4,5},{5,6},{6,7},{7,8},{8,9},{9,10},{10,1... | collective-permute-start | bytes 1572872 | tf_op jit(solution)/shard_map/ppermute | solution.py:28
  404.7 52.0 %all-reduce = (f32[128]{0:T(128)S(1)}, f32[128]{0:T(128)S(1)}) all-reduce(f32[128]{0:T(128)S(1)} %get-tuple-element.17, f32[128]{0:T(128)S(1)} %multiply_reduce_fusion.4), channel_id=1, replica_groups=mesh['gx'=4,'gy'=8] {'gx','gy'}, use_global_device_ids=true, to_apply=%region_4.6 | all-reduce | flops 256 | bytes 2048 | tf_op jit(solution)/shard_map/psum | solution.py:54
  459.7 41.2 %psum.81 = f32[128]{0:T(128)S(1)} all-reduce(f32[128]{0:T(128)S(1)} %get-tuple-element.13), channel_id=1, replica_groups=mesh['gx'=4,'gy'=8] {'gx','gy'}, use_global_device_ids=true, to_apply=%region_10.12 | all-reduce | flops 128 | bytes 1024 | tf_op jit(solution)/shard_map/psum | solution.py:54
  500.8 78.6 %all-reduce.11.cloned.1.call-done = f32[128,128]{0,1:T(8,128)} async-done(((f32[128,128]{0,1:T(8,128)}), f32[128,128]{0,1:T(8,128)}) %all-reduce.11.cloned.1.call-update) | async-done | bytes 65552 | tf_op jit(solution)/shard_map/psum | solution.py:54
  582.5 3.7 collective-permute-start.8
  587.7 3.1 collective-permute-done.9
  590.8 20.9 %fusion.14 = f32[2048,128]{0,1:T(8,128)} fusion(f32[1,2048,2048]{2,1,0:T(8,128)} %param.7, s32[]{:T(128)S(6)} %select_n.7, f32[1024,128]{0,1:T(8,128)S(1)} %collective-permute-done.8, f32[1024,128]{0,1:T(8,128)S(1)} %fusion.22, f32[1024,128]{0,1:T(8,128)S(1)} %collective-permute-done.9), kind=kOutput, calls=%fused_computation.10 | convolution fusion | flops 6442975232 | bytes 19398660 | tf_op jit(solution)/shard_map/dot_general | solution.py:36
  611.8 4.6 dynamic_update_slice.14
  617.8 13.9 %collective-permute-start.10 = (f32[1024,128]{0,1:T(8,128)S(1)}, f32[1024,128]{0,1:T(8,128)S(1)}, u32[]{:S(2)}, u32[]{:S(2)}) collective-permute-start(f32[1024,128]{0,1:T(8,128)S(1)} %get-tuple-element.21), channel_id=1, source_target_pairs={{0,1},{1,2},{2,3},{3,4},{4,5},{5,6},{6,7},{7,8},{8,9},{9,10},{10,1... | collective-permute-start | bytes 1572872 | tf_op jit(solution)/shard_map/ppermute | solution.py:28
  634.2 52.4 %psum.83 = f32[128]{0:T(128)S(1)} all-reduce(f32[128]{0:T(128)S(1)} %multiply_reduce_fusion.2), channel_id=1, replica_groups=mesh['gx'=4,'gy'=8] {'gx','gy'}, use_global_device_ids=true, to_apply=%region_14.16 | all-reduce | flops 128 | bytes 1024 | tf_op jit(solution)/shard_map/psum | solution.py:82
  691.3 40.6 %psum.84 = f32[128]{0:T(128)S(1)} all-reduce(f32[128]{0:T(128)S(1)} %get-tuple-element.9), channel_id=1, replica_groups=mesh['gx'=4,'gy'=8] {'gx','gy'}, use_global_device_ids=true, to_apply=%region_16.18 | all-reduce | flops 128 | bytes 1024 | tf_op jit(solution)/shard_map/psum | solution.py:54
  731.9 79.3 %all-reduce.13.cloned.1.call-done = f32[128,128]{0,1:T(8,128)} async-done(((f32[128,128]{0,1:T(8,128)}), f32[128,128]{0,1:T(8,128)}) %all-reduce.13.cloned.1.call-update) | async-done | bytes 65552 | tf_op jit(solution)/shard_map/psum | solution.py:54
  815.4 3.7 collective-permute-start.12
  820.6 3.0 collective-permute-done.13
  823.6 20.9 %fusion.17 = f32[2048,128]{0,1:T(8,128)} fusion(f32[1,2048,2048]{2,1,0:T(8,128)} %param.7, s32[]{:T(128)S(6)} %select_n.7, f32[1024,128]{0,1:T(8,128)S(1)} %collective-permute-done.12, f32[1024,128]{0,1:T(8,128)S(1)} %fusion.24, f32[1024,128]{0,1:T(8,128)S(1)} %collective-permute-done.13), kind=kOutput, calls=%fused_computation.11 | convolution fusion | flops 6442975232 | bytes 19398660 | tf_op jit(solution)/shard_map/dot_general | solution.py:36
  844.6 4.6 dynamic_update_slice.15
  850.8 13.9 %collective-permute-start.14 = (f32[1024,128]{0,1:T(8,128)S(1)}, f32[1024,128]{0,1:T(8,128)S(1)}, u32[]{:S(2)}, u32[]{:S(2)}) collective-permute-start(f32[1024,128]{0,1:T(8,128)S(1)} %get-tuple-element.19), channel_id=1, source_target_pairs={{0,1},{1,2},{2,3},{3,4},{4,5},{5,6},{6,7},{7,8},{8,9},{9,10},{10,1... | collective-permute-start | bytes 1572872 | tf_op jit(solution)/shard_map/ppermute | solution.py:28
  867.2 52.4 %psum.86 = f32[128]{0:T(128)S(1)} all-reduce(f32[128]{0:T(128)S(1)} %multiply_reduce_fusion), channel_id=1, replica_groups=mesh['gx'=4,'gy'=8] {'gx','gy'}, use_global_device_ids=true, to_apply=%region_20.22 | all-reduce | flops 128 | bytes 1024 | tf_op jit(solution)/shard_map/psum | solution.py:82
  919.6 2.7 convolution_bitcast_fusion.4
  924.8 117.5 %all-reduce.15.cloned.1.call-done = f32[128,128]{0,1:T(8,128)} async-done(((f32[128,128]{0,1:T(8,128)}), f32[128,128]{0,1:T(8,128)}) %all-reduce.15.cloned.1.call-update) | async-done | bytes 65552 | tf_op jit(solution)/shard_map/psum | solution.py:54
  (110 shorter events, 55.5 us)
Async XLA Ops:
  7.2 153.8 %copy-start.13 = (f32[128,128]{1,0:T(8,128)S(1)}, f32[128,128]{1,0:T(8,128)}, u32[]{:S(2)}) copy-start(f32[128,128]{1,0:T(8,128)} %param.11) | copy-start | bytes 196612
  7.2 129.1 %all-reduce.7.cloned.1.call-start = ((), (), s32[]{:S(2)}) async-start(), calls=%async_computation | async-start | bytes 131072 | tf_op jit(solution)/shard_map/psum | solution.py:71
  9.9 339.6 %all-reduce.9.cloned.1.call-start = ((), (), s32[]{:S(2)}) async-start(), calls=%async_computation.1 | async-start | bytes 131072 | tf_op jit(solution)/shard_map/psum | solution.py:54
  162.1 29.1 %copy-start.5 = (f32[1024,128]{0,1:T(8,128)}, f32[1024,128]{0,1:T(8,128)S(1)}, u32[]{:S(2)}) copy-start(f32[1024,128]{0,1:T(8,128)S(1)} %convolution_bitcast_fusion.3) | copy-start | bytes 1572868
  162.1 5.8 collective-permute-start
  165.8 4.6 collective-permute-start.1
  196.0 17.1 %copy-start.11 = (f32[1024,128]{1,0:T(8,128)S(1)}, f32[1024,128]{1,0:T(8,128)}, u32[]{:S(2)}) copy-start(f32[1024,128]{1,0:T(8,128)} %param.9) | copy-start | bytes 1572868
  197.0 16.2 %collective-permute-start.3 = (f32[1024,128]{0,1:T(8,128)}, f32[1024,128]{0,1:T(8,128)}, u32[]{:S(2)}, u32[]{:S(2)}) collective-permute-start(f32[1024,128]{0,1:T(8,128)} %get-tuple-element.26), channel_id=1, source_target_pairs={{1,0},{2,1},{3,2},{4,3},{5,4},{6,5},{7,6},{8,7},{9,8},{10,9},{11,1... | collective-permute-start | bytes 1572872 | tf_op jit(solution)/shard_map/ppermute | solution.py:28
  198.3 15.8 %collective-permute-start.2 = (f32[1024,128]{0,1:T(8,128)}, f32[1024,128]{0,1:T(8,128)}, u32[]{:S(2)}, u32[]{:S(2)}) collective-permute-start(f32[1024,128]{0,1:T(8,128)} %get-tuple-element.25), channel_id=1, source_target_pairs={{0,1},{1,2},{2,3},{3,4},{4,5},{5,6},{6,7},{7,8},{8,9},{9,10},{10,1... | collective-permute-start | bytes 1572872 | tf_op jit(solution)/shard_map/ppermute | solution.py:28
  215.5 136.0 %copy-start.4 = (f32[1024,128]{0,1:T(8,128)}, f32[1024,128]{0,1:T(8,128)S(1)}, u32[]{:S(2)}) copy-start(f32[1024,128]{0,1:T(8,128)S(1)} %get-tuple-element.18) | copy-start | bytes 1572868
  216.8 362.7 %all-reduce.11.cloned.1.call-start = ((), (), s32[]{:S(2)}) async-start(), calls=%async_computation.2 | async-start | bytes 131072 | tf_op jit(solution)/shard_map/psum | solution.py:54
  351.5 5.2 collective-permute-start.4
  355.2 4.6 collective-permute-start.5
  385.4 17.2 %copy-start.12 = (f32[128,128]{0,1:T(8,128)S(1)}, f32[128,128]{0,1:T(8,128)}, u32[]{:S(2)}) copy-start(f32[128,128]{0,1:T(8,128)} %all-reduce.9.cloned.1.call-done) | copy-start | bytes 196612
  386.4 16.2 %collective-permute-start.7 = (f32[1024,128]{0,1:T(8,128)}, f32[1024,128]{0,1:T(8,128)S(1)}, u32[]{:S(2)}, u32[]{:S(2)}) collective-permute-start(f32[1024,128]{0,1:T(8,128)} %get-tuple-element.24), channel_id=1, source_target_pairs={{1,0},{2,1},{3,2},{4,3},{5,4},{6,5},{7,6},{8,7},{9,8},{10,9},{11,1... | collective-permute-start | bytes 1572872 | tf_op jit(solution)/shard_map/ppermute | solution.py:28
  387.7 15.8 %collective-permute-start.6 = (f32[1024,128]{0,1:T(8,128)}, f32[1024,128]{0,1:T(8,128)}, u32[]{:S(2)}, u32[]{:S(2)}) collective-permute-start(f32[1024,128]{0,1:T(8,128)} %get-tuple-element.23), channel_id=1, source_target_pairs={{0,1},{1,2},{2,3},{3,4},{4,5},{5,6},{6,7},{7,8},{8,9},{9,10},{10,1... | collective-permute-start | bytes 1572872 | tf_op jit(solution)/shard_map/ppermute | solution.py:28
  402.7 54.0 %copy-start.6 = (f32[1024,128]{0,1:T(8,128)}, f32[1024,128]{0,1:T(8,128)S(1)}, u32[]{:S(2)}) copy-start(f32[1024,128]{0,1:T(8,128)S(1)} %collective-permute-done.7) | copy-start | bytes 1572868
  458.3 124.2 %copy-start.1 = (f32[1024,128]{0,1:T(8,128)}, f32[1024,128]{0,1:T(8,128)S(1)}, u32[]{:S(2)}) copy-start(f32[1024,128]{0,1:T(8,128)S(1)} %get-tuple-element.14) | copy-start | bytes 1572868
  459.6 351.6 %all-reduce.13.cloned.1.call-start = ((), (), s32[]{:S(2)}) async-start(), calls=%async_computation.3 | async-start | bytes 131072 | tf_op jit(solution)/shard_map/psum | solution.py:54
  582.5 5.1 collective-permute-start.8
  586.2 4.6 collective-permute-start.9
  616.5 15.3 %collective-permute-start.11 = (f32[1024,128]{0,1:T(8,128)S(1)}, f32[1024,128]{0,1:T(8,128)S(1)}, u32[]{:S(2)}, u32[]{:S(2)}) collective-permute-start(f32[1024,128]{0,1:T(8,128)S(1)} %get-tuple-element.22), channel_id=1, source_target_pairs={{1,0},{2,1},{3,2},{4,3},{5,4},{6,5},{7,6},{8,7},{9,8},{10,9},{11,1... | collective-permute-start | bytes 1572872 | tf_op jit(solution)/shard_map/ppermute | solution.py:28
  617.8 15.4 %collective-permute-start.10 = (f32[1024,128]{0,1:T(8,128)S(1)}, f32[1024,128]{0,1:T(8,128)S(1)}, u32[]{:S(2)}, u32[]{:S(2)}) collective-permute-start(f32[1024,128]{0,1:T(8,128)S(1)} %get-tuple-element.21), channel_id=1, source_target_pairs={{0,1},{1,2},{2,3},{3,4},{4,5},{5,6},{6,7},{7,8},{8,9},{9,10},{10,1... | collective-permute-start | bytes 1572872 | tf_op jit(solution)/shard_map/ppermute | solution.py:28
  631.7 1.5 copy-start.7
  691.3 351.0 %all-reduce.15.cloned.1.call-start = ((), (), s32[]{:S(2)}) async-start(), calls=%async_computation.4 | async-start | bytes 131072 | tf_op jit(solution)/shard_map/psum | solution.py:54
  815.4 29.1 %copy-start.2 = (f32[1024,128]{0,1:T(8,128)}, f32[1024,128]{0,1:T(8,128)S(1)}, u32[]{:S(2)}) copy-start(f32[1024,128]{0,1:T(8,128)S(1)} %fusion.24) | copy-start | bytes 1572868
  815.4 5.2 collective-permute-start.12
  819.0 4.6 collective-permute-start.13
  849.2 17.8 %copy-start.3 = (f32[1024,128]{0,1:T(8,128)S(1)}, f32[1024,128]{0,1:T(8,128)}, u32[]{:S(2)}) copy-start(f32[1024,128]{0,1:T(8,128)} %copy-done.2) | copy-start | bytes 1572868
  849.3 15.4 %collective-permute-start.15 = (f32[1024,128]{0,1:T(8,128)S(1)}, f32[1024,128]{0,1:T(8,128)S(1)}, u32[]{:S(2)}, u32[]{:S(2)}) collective-permute-start(f32[1024,128]{0,1:T(8,128)S(1)} %get-tuple-element.20), channel_id=1, source_target_pairs={{1,0},{2,1},{3,2},{4,3},{5,4},{6,5},{7,6},{8,7},{9,8},{10,9},{11,1... | collective-permute-start | bytes 1572872 | tf_op jit(solution)/shard_map/ppermute | solution.py:28
  850.8 15.4 %collective-permute-start.14 = (f32[1024,128]{0,1:T(8,128)S(1)}, f32[1024,128]{0,1:T(8,128)S(1)}, u32[]{:S(2)}, u32[]{:S(2)}) collective-permute-start(f32[1024,128]{0,1:T(8,128)S(1)} %get-tuple-element.19), channel_id=1, source_target_pairs={{0,1},{1,2},{2,3},{3,4},{4,5},{5,6},{6,7},{7,8},{8,9},{9,10},{10,1... | collective-permute-start | bytes 1572872 | tf_op jit(solution)/shard_map/ppermute | solution.py:28
  864.7 1.5 copy-start.9
  (3 other events, 2.7 us)
Sparse Core Ops, SparseCore 0:
  14.1 122.0 all-reduce.6
  216.9 132.5 all-reduce.8
  459.7 119.6 all-reduce.10
  691.4 119.8 all-reduce.12
  922.5 119.7 all-reduce.14
where the time goes:
time: 1060 us; the launch traced here: 1050 us
  waiting for transfers between devices  551 us (52%)
  blocking collectives  239 us (23%)
  matrix products  103 us (10%)
  starting transfers between devices  83.1 us (8%)
  other arithmetic  34 us (3%)
  local copies, waits for them, and re-layouts  26.2 us (2%)
  between operations  15.5 us (1%)
    psum x4, waiting for transfers between devices, project_sum(): lax.psum((local_coarse, jnp.sum(residual * residual, axis=0)), ('gx', 'gy'))  408 us
    psum x3, blocking collectives, project_sum(): lax.psum((local_coarse, jnp.sum(residual * residual, axis=0)), ('gx', 'gy'))  134 us
    psum x1, waiting for transfers between devices, local(): gram_matrix = lax.psum(local_gram, ('gx', 'gy'))  126 us
    psum x2, blocking collectives, local(): lax.psum(jnp.sum(direction * operator_image, axis=0), ('gx', 'gy'))  105 us
    dot_general x4, matrix products, apply_local(): jnp.dot(schur_block, window, precision=HIGHEST, preferred_element_type=jn...  83.5 us
    ppermute x8, starting transfers between devices, from_behind(): lax.ppermute(value, axis, [(source, source + steps) for source in range(i...  62.7 us
  transfers between devices with their start and end apart: 21, of which 15 were waited for; matrix products, arithmetic and copies ran while one was open for 0% of the time, Pallas kernels for 0%

commit v1 on v0

v1 whole, which is shorter than its diff:
```python
import jax
import jax.numpy as jnp
from jax import lax
from jax.experimental import pallas as pl
from jax.experimental.pallas import tpu as pltpu
from jax.sharding import PartitionSpec as P

ITERS = 3
AXES = ("gx", "gy")
HIGHEST = lax.Precision.HIGHEST
F32 = jnp.float32
BF16 = jnp.bfloat16
BLOCK = 256
MIB = 1 << 20


def dot(a, b):
    return jnp.dot(a, b, precision=HIGHEST, preferred_element_type=F32)


def dot_t(a, b):
    return lax.dot_general(
        a, b, (((0,), (0,)), ((), ())), precision=HIGHEST, preferred_element_type=F32
    )


def all_sum(value):
    count = lax.axis_size(AXES)
    bit = 1
    while bit < count:
        pairs = [(i, i ^ bit) for i in range(count)]
        value = value + lax.ppermute(value, AXES, pairs)
        bit *= 2
    return value


def swap(first, second):
    count = lax.axis_size(AXES)
    even, odd = [], []
    for i in range(0, count - 1, 2):
        even += [(i, i + 1), (i + 1, i)]
    for i in range(1, count - 1, 2):
        odd += [(i, i + 1), (i + 1, i)]
    return lax.ppermute(first, AXES, even), lax.ppermute(second, AXES, odd)


def fold(x):
    return jnp.sum(x.reshape(x.shape[0] // 8, 8, x.shape[1]), axis=0)


def total(x):
    return jnp.sum(x, axis=0, keepdims=True)


def product_kernel(meta, block, own, recv_e, recv_o, p_own, p_e, p_o, win, prod, quad, ext, cat, pext):
    step = pl.program_id(0)
    steps = pl.num_programs(0)
    slab, cols = own.shape
    reach = recv_e.shape[0]
    start = meta[0]
    even = meta[1]
    right = reach + slab
    e_at = pl.multiple_of(even * right, 8)
    o_at = pl.multiple_of((1 - even) * right, 8)
    rows = block.shape[1]

    @pl.when(step == 0)
    def _():
        ext[pl.ds(e_at, reach), :] = recv_e[...]
        ext[pl.ds(o_at, reach), :] = recv_o[...]
        ext[reach:right, :] = own[...]
        pext[...] = jnp.zeros(pext.shape, F32)
        quad[...] = jnp.zeros(quad.shape, F32)
        for j in range(win.shape[0] // BLOCK):
            chunk = ext[pl.ds(start + j * BLOCK, BLOCK), :]
            high = chunk.astype(BF16)
            low = (chunk - high.astype(F32)).astype(BF16)
            win[j * BLOCK : (j + 1) * BLOCK, :] = chunk
            cat[j * BLOCK : (j + 1) * BLOCK, :cols] = high
            cat[j * BLOCK : (j + 1) * BLOCK, cols:] = low

    a = block[0]
    a_high = a.astype(BF16)
    a_low = (a - a_high.astype(F32)).astype(BF16)
    wide = jnp.dot(a_high, cat[...], preferred_element_type=F32)
    narrow = jnp.dot(a_low, cat[:, :cols], preferred_element_type=F32)
    out = wide[:, :cols] + (wide[:, cols:] + narrow)
    at = pl.multiple_of(step * rows, rows)
    prod[pl.ds(at, rows), :] = out
    pext[pl.ds(start + at, rows), :] = out
    here = win[pl.ds(at, rows), :]
    if quad.shape[0] == 8:
        quad[...] += fold(here * out)
    else:
        quad[...] += dot_t(here, out)

    @pl.when(step == steps - 1)
    def _():
        p_own[...] = pext[reach:right, :]
        p_e[...] = pext[pl.ds(e_at, reach), :]
        p_o[...] = pext[pl.ds(o_at, reach), :]


def whole(shape):
    return pl.BlockSpec(shape, lambda *_: (0,) * len(shape))


def product(meta, schur, own, recv_e, recv_o, quad_rows):
    slab, cols = own.shape
    reach = recv_e.shape[0]
    window = schur.shape[1]
    span = 2 * reach + slab
    rows = BLOCK
    vec = lambda n: jax.ShapeDtypeStruct((n, cols), F32)
    outs = (vec(slab), vec(reach), vec(reach), vec(window), vec(window), vec(quad_rows))
    return pl.pallas_call(
        product_kernel,
        grid_spec=pltpu.PrefetchScalarGridSpec(
            num_scalar_prefetch=1,
            grid=(window // rows,),
            in_specs=[
                pl.BlockSpec((1, rows, window), lambda i, m: (0, i, 0)),
                whole((slab, cols)),
                whole((reach, cols)),
                whole((reach, cols)),
            ],
            out_specs=[whole(o.shape) for o in outs],
            scratch_shapes=[
                pltpu.VMEM((span, cols), F32),
                pltpu.VMEM((window, 2 * cols), BF16),
                pltpu.VMEM((span, cols), F32),
            ],
        ),
        out_shape=outs,
        compiler_params=pltpu.CompilerParams(
            dimension_semantics=("arbitrary",), vmem_limit_bytes=24 * MIB
        ),
        cost_estimate=pl.CostEstimate(
            flops=8 * window * window * cols, bytes_accessed=4 * window * window, transcendentals=0
        ),
        name="product",
    )(meta, schur, own, recv_e, recv_o)


def call(kernel, meta, args, shapes, name, limit=16):
    outs = tuple(jax.ShapeDtypeStruct(s, F32) for s in shapes)
    vmem = pl.BlockSpec(memory_space=pltpu.VMEM)
    return pl.pallas_call(
        kernel,
        in_specs=[pl.BlockSpec(memory_space=pltpu.SMEM)] + [vmem] * len(args),
        out_specs=[vmem] * len(outs),
        out_shape=outs,
        compiler_params=pltpu.CompilerParams(vmem_limit_bytes=limit * MIB),
        name=name,
    )(meta, *args)


def places(meta, slab, reach):
    base = slab - reach
    even = meta[1]
    return pl.multiple_of(even * base, 8), pl.multiple_of((1 - even) * base, 8)


def gather_rows(meta, dst, p_own, recv_e, recv_o):
    slab, reach = p_own.shape[0], recv_e.shape[0]
    e_at, o_at = places(meta, slab, reach)
    dst[...] = p_own[...]
    dst[pl.ds(e_at, reach), :] += recv_e[...]
    dst[pl.ds(o_at, reach), :] += recv_o[...]


def offer(meta, src, send_e, send_o):
    slab, reach = src.shape[0], send_e.shape[0]
    e_at, o_at = places(meta, slab, reach)
    send_e[...] = src[pl.ds(e_at, reach), :]
    send_o[...] = src[pl.ds(o_at, reach), :]


def begin_kernel(meta, basis, rhs, send_e, send_o, sums):
    nc = basis.shape[1]
    offer(meta, basis, send_e, send_o)
    b = basis[...]
    sums[:nc, :] = dot_t(b, b)
    sums[nc:, :] = dot_t(b, rhs[...])


def start_kernel(meta, p_own, recv_e, recv_o, basis, rhs, m_sum, b_sum, inverse, load,
                 c, lam, u, send_e, send_o, rho, sums):
    gather_rows(meta, c, p_own, recv_e, recv_o)
    y = dot(inverse[...], load[...])
    coarse = b_sum[...] - dot(m_sum[...], y)
    amp = dot(inverse[...], coarse)
    rho[...] = coarse
    lam[...] = dot(basis[...], y)
    u[...] = rhs[...] - dot(c[...], y) - dot(basis[...], amp)
    offer(meta, u, send_e, send_o)
    nc = basis.shape[1]
    sums[:nc, :] = dot_t(c[...], u[...])
    sums[nc:, :] = fold(u[...] * u[...])


def image_kernel(meta, p_own, recv_e, recv_o, c, w, send_e, send_o, more):
    gather_rows(meta, w, p_own, recv_e, recv_o)
    offer(meta, w, send_e, send_o)
    more[...] = dot_t(c[...], w[...])


def first_kernel(meta, p_own, recv_e, recv_o, basis, c, inverse, sums, u, w, lam, rho,
                 w1, send_e, send_o, lam1, u1, q0, rho1, amp0, scal, out):
    nc = basis.shape[1]
    gather_rows(meta, w1, p_own, recv_e, recv_o)
    k0 = sums[:nc, :]
    a0 = dot(inverse[...], k0)
    gamma = total(sums[2 * nc : 2 * nc + 8, :])
    curve = total(sums[2 * nc + 8 : 2 * nc + 16, :])
    alpha = gamma / curve
    w1[...] = w[...] - alpha * (w1[...] - dot(c[...], a0))
    offer(meta, w1, send_e, send_o)
    q0[...] = w[...] - dot(basis[...], a0)
    u1[...] = u[...] - alpha * q0[...]
    lam1[...] = lam[...] + alpha * u[...]
    rho1[...] = rho[...] - alpha * k0
    amp0[...] = a0
    scal[0:1, :] = gamma
    scal[1:2, :] = curve
    scal[2:3, :] = alpha
    scal[3:8, :] = jnp.zeros((5, scal.shape[1]), F32)
    out[:nc, :] = dot_t(c[...], u1[...])
    out[nc : 2 * nc, :] = dot_t(c[...], w1[...])
    out[2 * nc : 2 * nc + 8, :] = fold(u1[...] * u1[...])
    out[2 * nc + 8 : 2 * nc + 16, :] = fold(u1[...] * w1[...])
    out[2 * nc + 16 :, :] = fold(u1[...] * w[...])


def windows_kernel(meta, u_win, w_win, b_win, pu, pw, pb, amp0, scal, u1_win, q0_win, pu1, pq0):
    a0 = amp0[...]
    alpha = scal[2:3, :]
    q0_win[...] = w_win[...] - dot(b_win[...], a0)
    u1_win[...] = u_win[...] - alpha * q0_win[...]
    pq0[...] = pw[...] - dot(pb[...], a0)
    pu1[...] = pu[...] - alpha * pq0[...]


def second_kernel(meta, sums, inverse, m_sum, basis, u0, w0, w1, u1, q0, lam1, rho1, sums0, amp0, scal,
                  u1_win, q0_win, pu1, pq0, w1_win, pw1, b_win, pb,
                  lam2, u2, p1, rho2, k2, kk1, scal2, out):
    nc = basis.shape[1]
    k1 = sums[:nc, :]
    l1 = sums[nc : 2 * nc, :]
    gamma1 = total(sums[2 * nc : 2 * nc + 8, :])
    delta1 = total(sums[2 * nc + 8 : 2 * nc + 16, :])
    eps1 = total(sums[2 * nc + 16 :, :])
    gamma0 = scal[0:1, :]
    curve0 = scal[1:2, :]
    beta = gamma1 / gamma0
    curve = delta1 + beta * (2.0 * eps1 + beta * curve0)
    alpha = gamma1 / curve
    a1 = dot(inverse[...], k1)
    k0 = sums0[:nc, :]
    l0 = sums0[nc : 2 * nc, :]
    q1_win = w1_win[...] - dot(b_win[...], a1) + beta * q0_win[...]
    pq1 = pw1[...] - dot(pb[...], a1) + beta * pq0[...]
    u2_win = u1_win[...] - alpha * q1_win
    pu2 = pu1[...] - alpha * pq1
    q1 = w1[...] - dot(basis[...], a1) + beta * q0[...]
    u2[...] = u1[...] - alpha * q1
    s1 = w1[...] + beta * w0[...]
    out[0:8, :] = fold(u2[...] * u2[...])
    out[8:16, :] = fold(u2_win * pu2)
    out[16:24, :] = fold(u2[...] * s1)
    p1[...] = u1[...] + beta * u0[...]
    lam2[...] = lam1[...] + alpha * p1[...]
    kk1[...] = k1 + beta * k0
    rho2[...] = rho1[...] - alpha * kk1[...]
    cq0 = l0 - dot(m_sum[...], amp0[...])
    k2[...] = k1 - alpha * (l1 - dot(m_sum[...], a1) + beta * cq0)
    scal2[0:1, :] = gamma1
    scal2[1:2, :] = curve
    scal2[2:8, :] = jnp.zeros((6, scal2.shape[1]), F32)


def last_kernel(meta, sums, inverse, lam2, u2, p1, rho2, k2, kk1, scal2, lam, amp):
    gamma2 = total(sums[0:8, :])
    delta2 = total(sums[8:16, :])
    eps2 = total(sums[16:24, :])
    beta = gamma2 / scal2[0:1, :]
    curve = delta2 + beta * (2.0 * eps2 + beta * scal2[1:2, :])
    alpha = gamma2 / curve
    lam[...] = lam2[...] + alpha * (u2[...] + beta * p1[...])
    rho3 = rho2[...] - alpha * (k2[...] + beta * kk1[...])
    amp[...] = dot(inverse[...], rho3)


def local(schur, offsets, rhs, basis, load):
    slab, cols = rhs.shape
    nc = basis.shape[1]
    window = schur.shape[1]
    reach = 3 * slab // 4
    index = lax.axis_index(AXES)
    meta = jnp.stack([offsets[0] - (slab - reach), 1 - index % 2]).astype(jnp.int32)
    vec, hal, sml = (slab, cols), (reach, cols), (nc, cols)
    win = (window, cols)

    send_e, send_o, sums = call(begin_kernel, meta, (basis, rhs), (hal, hal, (2 * nc, cols)), "begin")
    recv = swap(send_e, send_o)
    gram_rhs = all_sum(sums)
    p_own, p_e, p_o, b_win, pb, m_local = product(meta, schur, basis, *recv, nc)
    recv = swap(p_e, p_o)
    m_sum = all_sum(m_local)
    factor = jnp.linalg.cholesky(gram_rhs[:nc])
    tri = lax.linalg.triangular_solve(factor, jnp.eye(nc, dtype=F32), left_side=True, lower=True)
    inverse = dot_t(tri, tri)
    c, lam0, u0, send_e, send_o, rho0, sums = call(
        start_kernel, meta, (p_own, *recv, basis, rhs, m_sum, gram_rhs[nc:], inverse, load),
        (vec, vec, vec, hal, hal, sml, (nc + 8, cols)), "start")
    recv = swap(send_e, send_o)
    p_own, p_e, p_o, u_win, pu, delta = product(meta, schur, u0, *recv, 8)
    recv = swap(p_e, p_o)
    w0, send_e, send_o, more = call(
        image_kernel, meta, (p_own, *recv, c), (vec, hal, hal, sml), "image")
    recv = swap(send_e, send_o)
    sums0 = all_sum(jnp.concatenate([sums[:nc], more, sums[nc:], delta], axis=0))
    p_own, p_e, p_o, w_win, pw, _ = product(meta, schur, w0, *recv, 8)
    recv = swap(p_e, p_o)
    big = (2 * nc + 24, cols)
    w1, send_e, send_o, lam1, u1, q0, rho1, amp0, scal, sums = call(
        first_kernel, meta, (p_own, *recv, basis, c, inverse, sums0, u0, w0, lam0, rho0),
        (vec, hal, hal, vec, vec, vec, sml, sml, (8, cols), big), "first")
    recv = swap(send_e, send_o)
    sums1 = all_sum(sums)
    u1_win, q0_win, pu1, pq0 = call(
        windows_kernel, meta, (u_win, w_win, b_win, pu, pw, pb, amp0, scal), (win,) * 4, "windows", 24)
    _, _, _, w1_win, pw1, _ = product(meta, schur, w1, *recv, 8)
    lam2, u2, p1, rho2, k2, kk1, scal2, sums = call(
        second_kernel, meta,
        (sums1, inverse, m_sum, basis, u0, w0, w1, u1, q0, lam1, rho1, sums0, amp0, scal,
         u1_win, q0_win, pu1, pq0, w1_win, pw1, b_win, pb),
        (vec, vec, vec, sml, sml, sml, (8, cols), (24, cols)), "second", 40)
    sums2 = all_sum(sums)
    lam, amp = call(
        last_kernel, meta, (sums2, inverse, lam2, u2, p1, rho2, k2, kk1, scal2), (vec, sml), "last")
    return lam, amp


def solution(mesh):
    in_specs = (P(AXES, None, None), P(AXES), P(AXES, None), P(AXES, None), P())
    out_specs = (P(AXES, None), P())
    return jax.shard_map(local, mesh=mesh, in_specs=in_specs, out_specs=out_specs, check_vma=False)
```

time: 1060 us -> 260 us (0.25)
  waiting for transfers between devices: 551 us -> 71.1 us
  blocking collectives: 239 us -> 0 us
  matrix products: 103 us -> 0.54 us
  Pallas kernels: 0 us -> 50.3 us
  between operations: 15.5 us -> 1.85 us
  starting transfers between devices: 83.1 us -> 72.1 us
  local copies, waits for them, and re-layouts: 26.2 us -> 36.9 us
    psum x5 -> x0, waiting for transfers between devices: 534 us -> none  [the longest x4 408 us: project_sum(): lax.psum((local_coarse, jnp.sum(residual * residual, axis=0)), ('gx', 'gy'))]
    psum x5 -> x0, blocking collectives: 239 us -> none  [the longest x3 134 us: project_sum(): lax.psum((local_coarse, jnp.sum(residual * residual, axis=0)), ('gx', 'gy'))]
    dot_general x13 -> x1, matrix products: 96.5 us -> 0.29 us  [dot_t(): lax.dot_general(a, b, (((0,), (0,)), ((), ())), precision=HIGHEST, prefer...]
    ppermute x16 -> x39, waiting for transfers between devices: 16.5 us -> 71.1 us  [the longest x25 69.4 us: all_sum(): value = value + lax.ppermute(value, AXES, pairs)]
    pallas_call x0 -> x11, Pallas kernels: none -> 50.3 us  [the longest x4 32.2 us: product(): pl.pallas_call(product_kernel, grid_spec=pltpu.PrefetchScalarGridSpec(num...]
    unnamed x30 -> x82, local copies, waits for them, and re-layouts: 3.84 us -> 36.8 us
    dynamic_update_slice x4 -> x0, local copies, waits for them, and re-layouts: 18.3 us -> none  [apply_local(): lax.dynamic_update_slice_in_dim(spread, product_block, start_row, 0)]
    ppermute x16 -> x39, starting transfers between devices: 82.9 us -> 72.1 us  [the longest x25 53 us: all_sum(): value = value + lax.ppermute(value, AXES, pairs)]
  transfers between devices with their start and end apart: 21 -> 39, of which waited for: 15 -> 18; matrix products, arithmetic and copies ran while one was open for 0% -> 10% of each run, Pallas kernels for 0% -> 11%
where the time goes in v1:
time: 260 us; the launch traced here: 258 us
  starting transfers between devices  72.1 us (28%)
  waiting for transfers between devices  71.1 us (27%)
  Pallas kernels  50.3 us (19%)
  local copies, waits for them, and re-layouts  36.9 us (14%)
  other arithmetic  25.6 us (10%)
    ppermute x25, waiting for transfers between devices, all_sum(): value = value + lax.ppermute(value, AXES, pairs)  69.4 us
    ppermute x25, starting transfers between devices, all_sum(): value = value + lax.ppermute(value, AXES, pairs)  53 us
    unnamed x82, local copies, waits for them, and re-layouts  36.8 us
    pallas_call x4, Pallas kernels, product(): pl.pallas_call(product_kernel, grid_spec=pltpu.PrefetchScalarGridSpec(num...  32.2 us
    ppermute x14, starting transfers between devices, swap(): return (lax.ppermute(first, AXES, even), lax.ppermute(second, AXES, odd))  19.1 us
    pallas_call x7, Pallas kernels, call(): pl.pallas_call(kernel, in_specs=[pl.BlockSpec(memory_space=pltpu.SMEM)] +...  18.2 us
    another operation x3, other arithmetic, local(): factor = jnp.linalg.cholesky(gram_rhs[:nc])  13.2 us
    another operation x2, other arithmetic, local(): lax.linalg.triangular_solve(factor, jnp.eye(nc, dtype=F32), left_side=Tru...  10.5 us
  transfers between devices with their start and end apart: 39, of which 18 were waited for; matrix products, arithmetic and copies ran while one was open for 10% of the time, Pallas kernels for 11%

profile of v1, /device:TPU:0, one launch (start us, length us, event | category | flops | bytes accessed | tf_op | source)
XLA Modules:
  0.0 258.4 jit_solution(13135722778565291651)
XLA Ops:
  6.3 4.0 %collective-permute-start.9 = (f32[256,128]{1,0:T(8,128)S(1)}, f32[256,128]{1,0:T(8,128)S(1)}, u32[]{:S(2)}, u32[]{:S(2)}) collective-permute-start(f32[256,128]{1,0:T(8,128)S(1)} %get-tuple-element.63), channel_id=1, source_target_pairs={{0,1},{1,0},{2,3},{3,2},{4,5},{5,4},{6,7},{7,6},{8,9},{9,8},{10,11... | collective-permute-start | bytes 393224 | tf_op jit(solution)/shard_map/ppermute | solution.py:32
  13.0 9.9 %collective-permute-done.10 = f32[256,128]{1,0:T(8,128)S(1)} collective-permute-done((f32[256,128]{1,0:T(8,128)S(1)}, f32[256,128]{1,0:T(8,128)S(1)}, u32[]{:S(2)}, u32[]{:S(2)}) %collective-permute-start.10) | collective-permute-done | bytes 131104 | tf_op jit(solution)/shard_map/ppermute | solution.py:32
  22.9 3.1 %collective-permute-start.11 = (f32[256,128]{1,0:T(8,128)S(1)}, f32[256,128]{1,0:T(8,128)S(1)}, u32[]{:S(2)}, u32[]{:S(2)}) collective-permute-start(f32[256,128]{1,0:T(8,128)S(1)} %add.103), channel_id=1, source_target_pairs={{0,4},{1,5},{2,6},{3,7},{4,0},{5,1},{6,2},{7,3},{8,12},{9,13},{10,... | collective-permute-start | bytes 393224 | tf_op jit(solution)/shard_map/ppermute | solution.py:32
  26.1 5.8 %copy-done = f32[1,2048,2048]{2,1,0:T(8,128)S(1)} copy-done((f32[1,2048,2048]{2,1,0:T(8,128)S(1)}, f32[1,2048,2048]{2,1,0:T(8,128)}, u32[]{:S(2)}) %copy-start) | copy-done | bytes 16777240
  32.9 9.8 %product.4 = (f32[1024,128]{1,0:T(8,128)S(1)}, f32[768,128]{1,0:T(8,128)}, f32[768,128]{1,0:T(8,128)}, f32[2048,128]{1,0:T(8,128)S(1)}, f32[2048,128]{1,0:T(8,128)S(1)}, /*index=5*/f32[128,128]{1,0:T(8,128)S(1)}) custom-call(s32[2]{0:T(128)S(1)} %pad_add_fusion.meta, f32[1,2048,2048]{2,1,0:T(8,128)S(1)} %copy-done, f32[1024,128]{1,0:T(8,128)S(1)} %copy-done.3, ...), custom_call_target="tpu_custom_call" | custom-call | flops 4294967296 | bytes 16777216 | tf_op jit(solution)/shard_map/product/pallas_call | solution.py:116
  45.7 3.8 %collective-permute-done.5 = f32[128,128]{1,0:T(8,128)S(1)} collective-permute-done((f32[128,128]{1,0:T(8,128)S(1)}, f32[128,128]{1,0:T(8,128)S(1)}, u32[]{:S(2)}, u32[]{:S(2)}) %collective-permute-start.5) | collective-permute-done | bytes 65568 | tf_op jit(solution)/shard_map/ppermute | solution.py:32
  51.2 4.1 %collective-permute-done.6 = f32[128,128]{1,0:T(8,128)S(1)} collective-permute-done((f32[128,128]{1,0:T(8,128)S(1)}, f32[128,128]{1,0:T(8,128)S(1)}, u32[]{:S(2)}, u32[]{:S(2)}) %collective-permute-start.6) | collective-permute-done | bytes 65568 | tf_op jit(solution)/shard_map/ppermute | solution.py:32
  62.2 12.5 %cholesky.17 = f32[128,128]{1,0:T(8,128)S(1)} custom-call(f32[128,128]{1,0:T(8,128)} %get-tuple-element.112), custom_call_target="Cholesky" | custom-call | tf_op jit(solution)/shard_map/jit(cholesky)/cholesky | solution.py:310
  76.1 9.8 %custom-call.6 = f32[1,128,128]{1,2,0:T(8,128)S(1)} custom-call(f32[1,128,128]{2,1,0:T(8,128)S(1)} %fusion), custom_call_target="InvertDiagBlocksLowerTriangular" | custom-call | tf_op jit(solution)/shard_map/triangular_solve | solution.py:311
  88.4 4.2 %start.1 = (f32[1024,128]{1,0:T(8,128)S(1)}, f32[1024,128]{1,0:T(8,128)S(1)}, f32[1024,128]{1,0:T(8,128)S(1)}, f32[768,128]{1,0:T(8,128)S(1)}, f32[768,128]{1,0:...) custom-call(s32[2]{0:T(128)S(1)} %pad_add_fusion.meta, f32[1024,128]{1,0:T(8,128)S(1)} %copy-done.35, ...), custom_call_target="tpu_custom_call" | custom-call | tf_op jit(solution)/shard_map/start/pallas_call | solution.py:148
  94.4 5.8 %copy-done.1 = f32[1,2048,2048]{2,1,0:T(8,128)S(1)} copy-done((f32[1,2048,2048]{2,1,0:T(8,128)S(1)}, f32[1,2048,2048]{2,1,0:T(8,128)}, u32[]{:S(2)}) %copy-start.1) | copy-done | bytes 16777240
  100.2 6.9 %product.5 = (f32[1024,128]{1,0:T(8,128)S(1)}, f32[768,128]{1,0:T(8,128)S(1)}, f32[768,128]{1,0:T(8,128)S(1)}, f32[2048,128]{1,0:T(8,128)S(1)}, f32[2048,128]{1,0:T(8,128)S(1)}, /*index=5*/f32[8,128]{1,0:T(8,128)S(1)}) custom-call(s32[2]{0:T(128)S(1)} %pad_add_fusion.meta, f32[1,2048,2048]{2,1,0:T(8,128)S(1)} %copy-done.1, ...), custom_call_target="tpu_custom_call" | custom-call | flops 4294967296 | bytes 16777216 | tf_op jit(solution)/shard_map/product/pallas_call | solution.py:116
  109.0 10.4 %collective-permute-start.16 = (f32[768,128]{1,0:T(8,128)S(1)}, f32[768,128]{1,0:T(8,128)S(1)}, u32[]{:S(2)}, u32[]{:S(2)}) collective-permute-start(f32[768,128]{1,0:T(8,128)S(1)} %get-tuple-element.68), channel_id=1, source_target_pairs={{0,1},{1,0},{2,3},{3,2},{4,5},{5,4},{6,7},{7,6},{8,9},{9,8},{10,11... | collective-permute-start | bytes 1179656 | tf_op jit(solution)/shard_map/ppermute | solution.py:44
  122.1 7.8 %collective-permute-start.22 = (f32[272,128]{1,0:T(8,128)S(1)}, f32[272,128]{1,0:T(8,128)S(1)}, u32[]{:S(2)}, u32[]{:S(2)}) collective-permute-start(f32[272,128]{1,0:T(8,128)S(1)} %pad_maximum_fusion), channel_id=1, source_target_pairs={{0,1},{1,0},{2,3},{3,2},{4,5},{5,4},{6,7},{7,6},{8,9},{9,8},{10,11... | collective-permute-start | bytes 417800 | tf_op jit(solution)/shard_map/ppermute | solution.py:32
  130.9 3.5 %collective-permute-start.23 = (f32[272,128]{1,0:T(8,128)S(1)}, f32[272,128]{1,0:T(8,128)S(1)}, u32[]{:S(2)}, u32[]{:S(2)}) collective-permute-start(f32[272,128]{1,0:T(8,128)S(1)} %fusion.4), channel_id=1, source_target_pairs={{0,2},{1,3},{2,0},{3,1},{4,6},{5,7},{6,4},{7,5},{8,10},{9,11},{10,... | collective-permute-start | bytes 417800 | tf_op jit(solution)/shard_map/ppermute | solution.py:32
  134.4 8.4 %collective-permute-done.23 = f32[272,128]{1,0:T(8,128)S(1)} collective-permute-done((f32[272,128]{1,0:T(8,128)S(1)}, f32[272,128]{1,0:T(8,128)S(1)}, u32[]{:S(2)}, u32[]{:S(2)}) %collective-permute-start.23) | collective-permute-done | bytes 139296 | tf_op jit(solution)/shard_map/ppermute | solution.py:32
  142.8 10.2 %collective-permute-start.24 = (f32[272,128]{1,0:T(8,128)S(1)}, f32[272,128]{1,0:T(8,128)S(1)}, u32[]{:S(2)}, u32[]{:S(2)}) collective-permute-start(f32[272,128]{1,0:T(8,128)S(1)} %add.109), channel_id=1, source_target_pairs={{0,4},{1,5},{2,6},{3,7},{4,0},{5,1},{6,2},{7,3},{8,12},{9,13},{10,... | collective-permute-start | bytes 417800 | tf_op jit(solution)/shard_map/ppermute | solution.py:32
  153.1 7.5 %product.6 = (f32[1024,128]{1,0:T(8,128)S(1)}, f32[768,128]{1,0:T(8,128)S(1)}, f32[768,128]{1,0:T(8,128)S(1)}, f32[2048,128]{1,0:T(8,128)S(1)}, f32[2048,128]{1,0:T(8,128)S(1)}, /*index=5*/f32[8,128]{1,0:T(8,128)}) custom-call(s32[2]{0:T(128)S(1)} %pad_add_fusion.meta, f32[1,2048,2048]{2,1,0:T(8,128)S(1)} %copy-done.1, ...), custom_call_target="tpu_custom_call" | custom-call | flops 4294967296 | bytes 16777216 | tf_op jit(solution)/shard_map/product/pallas_call | solution.py:116
  160.5 2.1 collective-permute-start.20
  163.4 2.2 collective-permute-start.25
  165.6 3.7 %collective-permute-done.25 = f32[272,128]{1,0:T(8,128)S(1)} collective-permute-done((f32[272,128]{1,0:T(8,128)S(1)}, f32[272,128]{1,0:T(8,128)S(1)}, u32[]{:S(2)}, u32[]{:S(2)}) %collective-permute-start.25) | collective-permute-done | bytes 139296 | tf_op jit(solution)/shard_map/ppermute | solution.py:32
  169.3 5.0 %collective-permute-start.26 = (f32[272,128]{1,0:T(8,128)S(1)}, f32[272,128]{1,0:T(8,128)S(1)}, u32[]{:S(2)}, u32[]{:S(2)}) collective-permute-start(f32[272,128]{1,0:T(8,128)S(1)} %add.111), channel_id=1, source_target_pairs={{0,16},{1,17},{2,18},{3,19},{4,20},{5,21},{6,22},{7,23},{8,24},{9,... | collective-permute-start | bytes 417800 | tf_op jit(solution)/shard_map/ppermute | solution.py:32
  174.3 3.9 %collective-permute-done.26 = f32[272,128]{1,0:T(8,128)S(1)} collective-permute-done((f32[272,128]{1,0:T(8,128)S(1)}, f32[272,128]{1,0:T(8,128)S(1)}, u32[]{:S(2)}, u32[]{:S(2)}) %collective-permute-start.26) | collective-permute-done | bytes 139296 | tf_op jit(solution)/shard_map/ppermute | solution.py:32
  179.3 3.2 %first.1 = (f32[1024,128]{1,0:T(8,128)S(1)}, f32[768,128]{1,0:T(8,128)S(1)}, f32[768,128]{1,0:T(8,128)S(1)}, f32[1024,128]{1,0:T(8,128)S(1)}, f32[1024,128]{1,0:...) custom-call(s32[2]{0:T(128)S(1)} %pad_add_fusion.meta, ...), custom_call_target="tpu_custom_call" | custom-call | tf_op jit(solution)/shard_map/first/pallas_call | solution.py:148
  185.7 4.9 %collective-permute-done.28 = f32[280,128]{1,0:T(8,128)S(1)} collective-permute-done((f32[280,128]{1,0:T(8,128)S(1)}, f32[280,128]{1,0:T(8,128)S(1)}, u32[]{:S(2)}, u32[]{:S(2)}) %collective-permute-start.28) | collective-permute-done | bytes 143392 | tf_op jit(solution)/shard_map/ppermute | solution.py:32
  190.6 4.0 %collective-permute-start.29 = (f32[280,128]{1,0:T(8,128)S(1)}, f32[280,128]{1,0:T(8,128)S(1)}, u32[]{:S(2)}, u32[]{:S(2)}) collective-permute-start(f32[280,128]{1,0:T(8,128)S(1)} %add.114), channel_id=1, source_target_pairs={{0,4},{1,5},{2,6},{3,7},{4,0},{5,1},{6,2},{7,3},{8,12},{9,13},{10,... | collective-permute-start | bytes 430088 | tf_op jit(solution)/shard_map/ppermute | solution.py:32
  194.7 13.1 %collective-permute-done.29 = f32[280,128]{1,0:T(8,128)S(1)} collective-permute-done((f32[280,128]{1,0:T(8,128)S(1)}, f32[280,128]{1,0:T(8,128)S(1)}, u32[]{:S(2)}, u32[]{:S(2)}) %collective-permute-start.29) | collective-permute-done | bytes 143392 | tf_op jit(solution)/shard_map/ppermute | solution.py:32
  212.2 2.6 windows.1
  215.4 8.0 %product.7 = (f32[1024,128]{1,0:T(8,128)}, f32[768,128]{1,0:T(8,128)}, f32[768,128]{1,0:T(8,128)}, f32[2048,128]{1,0:T(8,128)S(1)}, f32[2048,128]{1,0:T(8,128)S(1)}, /*index=5*/f32[8,128]{1,0:T(8,128)}) custom-call(s32[2]{0:T(128)S(1)} %pad_add_fusion.meta, f32[1,2048,2048]{2,1,0:T(8,128)S(1)} %bitcast.13, f32[1024,128]{1,0:T(8,128)S(1)} %get-tuple-element.83.own.w1, ...), custom_call_target="tpu_custom_call" | custom-call | flops 4294967296 | bytes 16777216 | tf_op jit(solution)/shard_map/product/pallas_call | solution.py:116
  236.2 3.6 %second.1 = (f32[1024,128]{1,0:T(8,128)S(1)}, f32[1024,128]{1,0:T(8,128)S(1)}, f32[1024,128]{1,0:T(8,128)S(1)}, f32[128,128]{1,0:T(8,128)S(1)}, f32[128,128]{1,0...) custom-call(s32[2]{0:T(128)S(1)} %pad_add_fusion.meta, ...), custom_call_target="tpu_custom_call" | custom-call | tf_op jit(solution)/shard_map/second/pallas_call | solution.py:148
  241.0 3.7 %collective-permute-done.35 = f32[24,128]{1,0:T(8,128)S(1)} collective-permute-done((f32[24,128]{1,0:T(8,128)S(1)}, f32[24,128]{1,0:T(8,128)S(1)}, u32[]{:S(2)}, u32[]{:S(2)}) %collective-permute-start.35) | collective-permute-done | bytes 12320 | tf_op jit(solution)/shard_map/ppermute | solution.py:32
  244.7 4.6 %collective-permute-done.36 = f32[24,128]{1,0:T(8,128)S(1)} collective-permute-done((f32[24,128]{1,0:T(8,128)S(1)}, f32[24,128]{1,0:T(8,128)S(1)}, u32[]{:S(2)}, u32[]{:S(2)}) %collective-permute-start.36) | collective-permute-done | bytes 12320 | tf_op jit(solution)/shard_map/ppermute | solution.py:32
  (179 shorter events, 64.5 us)
Async XLA Ops:
  5.1 21.0 %collective-permute-start = (f32[768,128]{1,0:T(8,128)S(1)}, f32[768,128]{1,0:T(8,128)S(1)}, u32[]{:S(2)}, u32[]{:S(2)}) collective-permute-start(f32[768,128]{1,0:T(8,128)S(1)} %get-tuple-element.57), channel_id=1, source_target_pairs={{0,1},{1,0},{2,3},{3,2},{4,5},{5,4},{6,7},{7,6},{8,9},{9,8},{10,11... | collective-permute-start | bytes 1179656 | tf_op jit(solution)/shard_map/ppermute | solution.py:44
  5.7 20.4 %collective-permute-start.1 = (f32[768,128]{1,0:T(8,128)S(1)}, f32[768,128]{1,0:T(8,128)S(1)}, u32[]{:S(2)}, u32[]{:S(2)}) collective-permute-start(f32[768,128]{1,0:T(8,128)S(1)} %get-tuple-element.58), channel_id=1, source_target_pairs={{1,2},{2,1},{3,4},{4,3},{5,6},{6,5},{7,8},{8,7},{9,10},{10,9},{11,... | collective-permute-start | bytes 1179656 | tf_op jit(solution)/shard_map/ppermute | solution.py:44
  6.3 5.0 %collective-permute-start.9 = (f32[256,128]{1,0:T(8,128)S(1)}, f32[256,128]{1,0:T(8,128)S(1)}, u32[]{:S(2)}, u32[]{:S(2)}) collective-permute-start(f32[256,128]{1,0:T(8,128)S(1)} %get-tuple-element.63), channel_id=1, source_target_pairs={{0,1},{1,0},{2,3},{3,2},{4,5},{5,4},{6,7},{7,6},{8,9},{9,8},{10,11... | collective-permute-start | bytes 393224 | tf_op jit(solution)/shard_map/ppermute | solution.py:32
  11.3 11.6 %collective-permute-start.10 = (f32[256,128]{1,0:T(8,128)S(1)}, f32[256,128]{1,0:T(8,128)S(1)}, u32[]{:S(2)}, u32[]{:S(2)}) collective-permute-start(f32[256,128]{1,0:T(8,128)S(1)} %add.102), channel_id=1, source_target_pairs={{0,2},{1,3},{2,0},{3,1},{4,6},{5,7},{6,4},{7,5},{8,10},{9,11},{10,... | collective-permute-start | bytes 393224 | tf_op jit(solution)/shard_map/ppermute | solution.py:32
  22.9 20.6 %collective-permute-start.11 = (f32[256,128]{1,0:T(8,128)S(1)}, f32[256,128]{1,0:T(8,128)S(1)}, u32[]{:S(2)}, u32[]{:S(2)}) collective-permute-start(f32[256,128]{1,0:T(8,128)S(1)} %add.103), channel_id=1, source_target_pairs={{0,4},{1,5},{2,6},{3,7},{4,0},{5,1},{6,2},{7,3},{8,12},{9,13},{10,... | collective-permute-start | bytes 393224 | tf_op jit(solution)/shard_map/ppermute | solution.py:32
  43.5 6.4 %collective-permute-start.12 = (f32[256,128]{1,0:T(8,128)S(1)}, f32[256,128]{1,0:T(8,128)S(1)}, u32[]{:S(2)}, u32[]{:S(2)}) collective-permute-start(f32[256,128]{1,0:T(8,128)S(1)} %add.104), channel_id=1, source_target_pairs={{0,8},{1,9},{2,10},{3,11},{4,12},{5,13},{6,14},{7,15},{8,0},{9,1},... | collective-permute-start | bytes 393224 | tf_op jit(solution)/shard_map/ppermute | solution.py:32
  45.1 4.3 %collective-permute-start.5 = (f32[128,128]{1,0:T(8,128)S(1)}, f32[128,128]{1,0:T(8,128)S(1)}, u32[]{:S(2)}, u32[]{:S(2)}) collective-permute-start(f32[128,128]{1,0:T(8,128)S(1)} %add.97), channel_id=1, source_target_pairs={{0,2},{1,3},{2,0},{3,1},{4,6},{5,7},{6,4},{7,5},{8,10},{9,11},{10,... | collective-permute-start | bytes 196616 | tf_op jit(solution)/shard_map/ppermute | solution.py:32
  49.5 5.8 %collective-permute-start.6 = (f32[128,128]{1,0:T(8,128)S(1)}, f32[128,128]{1,0:T(8,128)S(1)}, u32[]{:S(2)}, u32[]{:S(2)}) collective-permute-start(f32[128,128]{1,0:T(8,128)S(1)} %add.98), channel_id=1, source_target_pairs={{0,4},{1,5},{2,6},{3,7},{4,0},{5,1},{6,2},{7,3},{8,12},{9,13},{10,... | collective-permute-start | bytes 196616 | tf_op jit(solution)/shard_map/ppermute | solution.py:32
  50.0 11.5 %collective-permute-start.13 = (f32[256,128]{1,0:T(8,128)S(1)}, f32[256,128]{1,0:T(8,128)S(1)}, u32[]{:S(2)}, u32[]{:S(2)}) collective-permute-start(f32[256,128]{1,0:T(8,128)S(1)} %add.105), channel_id=1, source_target_pairs={{0,16},{1,17},{2,18},{3,19},{4,20},{5,21},{6,22},{7,23},{8,24},{9,... | collective-permute-start | bytes 393224 | tf_op jit(solution)/shard_map/ppermute | solution.py:32
  55.3 4.3 %collective-permute-start.7 = (f32[128,128]{1,0:T(8,128)S(1)}, f32[128,128]{1,0:T(8,128)S(1)}, u32[]{:S(2)}, u32[]{:S(2)}) collective-permute-start(f32[128,128]{1,0:T(8,128)S(1)} %add.99), channel_id=1, source_target_pairs={{0,8},{1,9},{2,10},{3,11},{4,12},{5,13},{6,14},{7,15},{8,0},{9,1},... | collective-permute-start | bytes 196616 | tf_op jit(solution)/shard_map/ppermute | solution.py:32
  56.3 31.0 %collective-permute-start.2 = (f32[768,128]{1,0:T(8,128)}, f32[768,128]{1,0:T(8,128)}, u32[]{:S(2)}, u32[]{:S(2)}) collective-permute-start(f32[768,128]{1,0:T(8,128)} %get-tuple-element.60), channel_id=1, source_target_pairs={{0,1},{1,0},{2,3},{3,2},{4,5},{5,4},{6,7},{7,6},{8,9},{9,8},{10,11... | collective-permute-start | bytes 1179656 | tf_op jit(solution)/shard_map/ppermute | solution.py:44
  56.3 31.0 %collective-permute-start.3 = (f32[768,128]{1,0:T(8,128)}, f32[768,128]{1,0:T(8,128)}, u32[]{:S(2)}, u32[]{:S(2)}) collective-permute-start(f32[768,128]{1,0:T(8,128)} %get-tuple-element.61), channel_id=1, source_target_pairs={{1,2},{2,1},{3,4},{4,3},{5,6},{6,5},{7,8},{8,7},{9,10},{10,9},{11,... | collective-permute-start | bytes 1179656 | tf_op jit(solution)/shard_map/ppermute | solution.py:44
  59.7 26.8 %collective-permute-start.8 = (f32[128,128]{1,0:T(8,128)S(1)}, f32[128,128]{1,0:T(8,128)}, u32[]{:S(2)}, u32[]{:S(2)}) collective-permute-start(f32[128,128]{1,0:T(8,128)S(1)} %add.100), channel_id=1, source_target_pairs={{0,16},{1,17},{2,18},{3,19},{4,20},{5,21},{6,22},{7,23},{8,24},{9,... | collective-permute-start | bytes 196616 | tf_op jit(solution)/shard_map/ppermute | solution.py:32
  109.0 11.7 %collective-permute-start.16 = (f32[768,128]{1,0:T(8,128)S(1)}, f32[768,128]{1,0:T(8,128)S(1)}, u32[]{:S(2)}, u32[]{:S(2)}) collective-permute-start(f32[768,128]{1,0:T(8,128)S(1)} %get-tuple-element.68), channel_id=1, source_target_pairs={{0,1},{1,0},{2,3},{3,2},{4,5},{5,4},{6,7},{7,6},{8,9},{9,8},{10,11... | collective-permute-start | bytes 1179656 | tf_op jit(solution)/shard_map/ppermute | solution.py:44
  122.1 8.8 %collective-permute-start.22 = (f32[272,128]{1,0:T(8,128)S(1)}, f32[272,128]{1,0:T(8,128)S(1)}, u32[]{:S(2)}, u32[]{:S(2)}) collective-permute-start(f32[272,128]{1,0:T(8,128)S(1)} %pad_maximum_fusion), channel_id=1, source_target_pairs={{0,1},{1,0},{2,3},{3,2},{4,5},{5,4},{6,7},{7,6},{8,9},{9,8},{10,11... | collective-permute-start | bytes 417800 | tf_op jit(solution)/shard_map/ppermute | solution.py:32
  129.9 23.1 %collective-permute-start.18 = (f32[768,128]{1,0:T(8,128)S(1)}, f32[768,128]{1,0:T(8,128)S(1)}, u32[]{:S(2)}, u32[]{:S(2)}) collective-permute-start(f32[768,128]{1,0:T(8,128)S(1)} %get-tuple-element.72), channel_id=1, source_target_pairs={{0,1},{1,0},{2,3},{3,2},{4,5},{5,4},{6,7},{7,6},{8,9},{9,8},{10,11... | collective-permute-start | bytes 1179656 | tf_op jit(solution)/shard_map/ppermute | solution.py:44
  130.0 23.1 %collective-permute-start.19 = (f32[768,128]{1,0:T(8,128)S(1)}, f32[768,128]{1,0:T(8,128)S(1)}, u32[]{:S(2)}, u32[]{:S(2)}) collective-permute-start(f32[768,128]{1,0:T(8,128)S(1)} %get-tuple-element.73), channel_id=1, source_target_pairs={{1,2},{2,1},{3,4},{4,3},{5,6},{6,5},{7,8},{8,7},{9,10},{10,9},{11,... | collective-permute-start | bytes 1179656 | tf_op jit(solution)/shard_map/ppermute | solution.py:44
  130.9 11.9 %collective-permute-start.23 = (f32[272,128]{1,0:T(8,128)S(1)}, f32[272,128]{1,0:T(8,128)S(1)}, u32[]{:S(2)}, u32[]{:S(2)}) collective-permute-start(f32[272,128]{1,0:T(8,128)S(1)} %fusion.4), channel_id=1, source_target_pairs={{0,2},{1,3},{2,0},{3,1},{4,6},{5,7},{6,4},{7,5},{8,10},{9,11},{10,... | collective-permute-start | bytes 417800 | tf_op jit(solution)/shard_map/ppermute | solution.py:32
  142.8 20.5 %collective-permute-start.24 = (f32[272,128]{1,0:T(8,128)S(1)}, f32[272,128]{1,0:T(8,128)S(1)}, u32[]{:S(2)}, u32[]{:S(2)}) collective-permute-start(f32[272,128]{1,0:T(8,128)S(1)} %add.109), channel_id=1, source_target_pairs={{0,4},{1,5},{2,6},{3,7},{4,0},{5,1},{6,2},{7,3},{8,12},{9,13},{10,... | collective-permute-start | bytes 417800 | tf_op jit(solution)/shard_map/ppermute | solution.py:32
  160.5 17.7 %collective-permute-start.20 = (f32[768,128]{1,0:T(8,128)S(1)}, f32[768,128]{1,0:T(8,128)S(1)}, u32[]{:S(2)}, u32[]{:S(2)}) collective-permute-start(f32[768,128]{1,0:T(8,128)S(1)} %get-tuple-element.75), channel_id=1, source_target_pairs={{0,1},{1,0},{2,3},{3,2},{4,5},{5,4},{6,7},{7,6},{8,9},{9,8},{10,11... | collective-permute-start | bytes 1179656 | tf_op jit(solution)/shard_map/ppermute | solution.py:44
  162.6 15.6 %collective-permute-start.21 = (f32[768,128]{1,0:T(8,128)S(1)}, f32[768,128]{1,0:T(8,128)S(1)}, u32[]{:S(2)}, u32[]{:S(2)}) collective-permute-start(f32[768,128]{1,0:T(8,128)S(1)} %get-tuple-element.76), channel_id=1, source_target_pairs={{1,2},{2,1},{3,4},{4,3},{5,6},{6,5},{7,8},{8,7},{9,10},{10,9},{11,... | collective-permute-start | bytes 1179656 | tf_op jit(solution)/shard_map/ppermute | solution.py:44
  163.4 5.9 %collective-permute-start.25 = (f32[272,128]{1,0:T(8,128)S(1)}, f32[272,128]{1,0:T(8,128)S(1)}, u32[]{:S(2)}, u32[]{:S(2)}) collective-permute-start(f32[272,128]{1,0:T(8,128)S(1)} %add.110), channel_id=1, source_target_pairs={{0,8},{1,9},{2,10},{3,11},{4,12},{5,13},{6,14},{7,15},{8,0},{9,1},... | collective-permute-start | bytes 417800 | tf_op jit(solution)/shard_map/ppermute | solution.py:32
  169.3 8.9 %collective-permute-start.26 = (f32[272,128]{1,0:T(8,128)S(1)}, f32[272,128]{1,0:T(8,128)S(1)}, u32[]{:S(2)}, u32[]{:S(2)}) collective-permute-start(f32[272,128]{1,0:T(8,128)S(1)} %add.111), channel_id=1, source_target_pairs={{0,16},{1,17},{2,18},{3,19},{4,20},{5,21},{6,22},{7,23},{8,24},{9,... | collective-permute-start | bytes 417800 | tf_op jit(solution)/shard_map/ppermute | solution.py:32
  184.7 5.9 %collective-permute-start.28 = (f32[280,128]{1,0:T(8,128)S(1)}, f32[280,128]{1,0:T(8,128)S(1)}, u32[]{:S(2)}, u32[]{:S(2)}) collective-permute-start(f32[280,128]{1,0:T(8,128)S(1)} %add.113), channel_id=1, source_target_pairs={{0,2},{1,3},{2,0},{3,1},{4,6},{5,7},{6,4},{7,5},{8,10},{9,11},{10,... | collective-permute-start | bytes 430088 | tf_op jit(solution)/shard_map/ppermute | solution.py:32
  184.8 30.5 %collective-permute-start.32 = (f32[768,128]{1,0:T(8,128)S(1)}, f32[768,128]{1,0:T(8,128)S(1)}, u32[]{:S(2)}, u32[]{:S(2)}) collective-permute-start(f32[768,128]{1,0:T(8,128)S(1)} %get-tuple-element.100), channel_id=1, source_target_pairs={{0,1},{1,0},{2,3},{3,2},{4,5},{5,4},{6,7},{7,6},{8,9},{9,8},{10,11... | collective-permute-start | bytes 1179656 | tf_op jit(solution)/shard_map/ppermute | solution.py:44
  185.0 30.3 %collective-permute-start.33 = (f32[768,128]{1,0:T(8,128)S(1)}, f32[768,128]{1,0:T(8,128)S(1)}, u32[]{:S(2)}, u32[]{:S(2)}) collective-permute-start(f32[768,128]{1,0:T(8,128)S(1)} %get-tuple-element.101), channel_id=1, source_target_pairs={{1,2},{2,1},{3,4},{4,3},{5,6},{6,5},{7,8},{8,7},{9,10},{10,9},{11,... | collective-permute-start | bytes 1179656 | tf_op jit(solution)/shard_map/ppermute | solution.py:44
  190.6 17.1 %collective-permute-start.29 = (f32[280,128]{1,0:T(8,128)S(1)}, f32[280,128]{1,0:T(8,128)S(1)}, u32[]{:S(2)}, u32[]{:S(2)}) collective-permute-start(f32[280,128]{1,0:T(8,128)S(1)} %add.114), channel_id=1, source_target_pairs={{0,4},{1,5},{2,6},{3,7},{4,0},{5,1},{6,2},{7,3},{8,12},{9,13},{10,... | collective-permute-start | bytes 430088 | tf_op jit(solution)/shard_map/ppermute | solution.py:32
  207.8 7.0 %collective-permute-start.30 = (f32[280,128]{1,0:T(8,128)S(1)}, f32[280,128]{1,0:T(8,128)S(1)}, u32[]{:S(2)}, u32[]{:S(2)}) collective-permute-start(f32[280,128]{1,0:T(8,128)S(1)} %add.115), channel_id=1, source_target_pairs={{0,8},{1,9},{2,10},{3,11},{4,12},{5,13},{6,14},{7,15},{8,0},{9,1},... | collective-permute-start | bytes 430088 | tf_op jit(solution)/shard_map/ppermute | solution.py:32
  214.8 10.7 %collective-permute-start.31 = (f32[280,128]{1,0:T(8,128)S(1)}, f32[280,128]{1,0:T(8,128)S(1)}, u32[]{:S(2)}, u32[]{:S(2)}) collective-permute-start(f32[280,128]{1,0:T(8,128)S(1)} %add.116), channel_id=1, source_target_pairs={{0,16},{1,17},{2,18},{3,19},{4,20},{5,21},{6,22},{7,23},{8,24},{9,... | collective-permute-start | bytes 430088 | tf_op jit(solution)/shard_map/ppermute | solution.py:32
  241.0 3.7 %collective-permute-start.35 = (f32[24,128]{1,0:T(8,128)S(1)}, f32[24,128]{1,0:T(8,128)S(1)}, u32[]{:S(2)}, u32[]{:S(2)}) collective-permute-start(f32[24,128]{1,0:T(8,128)S(1)} %add.118), channel_id=1, source_target_pairs={{0,2},{1,3},{2,0},{3,1},{4,6},{5,7},{6,4},{7,5},{8,10},{9,11},{10,... | collective-permute-start | bytes 36872 | tf_op jit(solution)/shard_map/ppermute | solution.py:32
  244.7 4.6 %collective-permute-start.36 = (f32[24,128]{1,0:T(8,128)S(1)}, f32[24,128]{1,0:T(8,128)S(1)}, u32[]{:S(2)}, u32[]{:S(2)}) collective-permute-start(f32[24,128]{1,0:T(8,128)S(1)} %add.119), channel_id=1, source_target_pairs={{0,4},{1,5},{2,6},{3,7},{4,0},{5,1},{6,2},{7,3},{8,12},{9,13},{10,... | collective-permute-start | bytes 36872 | tf_op jit(solution)/shard_map/ppermute | solution.py:32
  249.3 3.7 %collective-permute-start.37 = (f32[24,128]{1,0:T(8,128)S(1)}, f32[24,128]{1,0:T(8,128)S(1)}, u32[]{:S(2)}, u32[]{:S(2)}) collective-permute-start(f32[24,128]{1,0:T(8,128)S(1)} %add.120), channel_id=1, source_target_pairs={{0,8},{1,9},{2,10},{3,11},{4,12},{5,13},{6,14},{7,15},{8,0},{9,1},... | collective-permute-start | bytes 36872 | tf_op jit(solution)/shard_map/ppermute | solution.py:32
  (48 other events, 733.9 us)

commit v2 on v0

v2 whole, which is shorter than its diff:
```python
import jax
import jax.numpy as jnp
from jax import lax
from jax.experimental import pallas as pl
from jax.experimental.pallas import tpu as pltpu
from jax.sharding import PartitionSpec as P


AXES = ("gx", "gy")
HIGHEST = lax.Precision.HIGHEST
F32 = jnp.float32
BF16 = jnp.bfloat16
BLOCK = 256
MIB = 1 << 20


def dot(a, b):
    return jnp.dot(a, b, precision=HIGHEST, preferred_element_type=F32)


def dot_t(a, b):
    return lax.dot_general(
        a, b, (((0,), (0,)), ((), ())), precision=HIGHEST, preferred_element_type=F32
    )


def exchange_sum(value, bits):
    count = lax.axis_size(AXES)
    masks = [0]
    for bit in bits:
        masks += [mask | bit for mask in masks]
    out = value
    for mask in masks[1:]:
        out = out + lax.ppermute(value, AXES, [(j, j ^ mask) for j in range(count)])
    return out


def groups(count):
    bits = [1 << i for i in range(1, count.bit_length() - 1)]
    return [bits[i : i + 2] for i in range(0, len(bits), 2)][::-1]


def core_sum(value):
    return exchange_sum(value, [1])


def core_swap(value):
    count = lax.axis_size(AXES)
    return lax.ppermute(value, AXES, [(i, i ^ 1) for i in range(count)])


def far_sum(value):
    for group in groups(lax.axis_size(AXES))[:-1]:
        value = exchange_sum(value, group)
    return value


def near_sum(value):
    last = groups(lax.axis_size(AXES))[-1]
    return exchange_sum(value, last)


def swap(first, second):
    count = lax.axis_size(AXES)
    even, odd = [], []
    for i in range(0, count - 1, 2):
        even += [(i, i + 1), (i + 1, i)]
    for i in range(1, count - 1, 2):
        odd += [(i, i + 1), (i + 1, i)]
    second = lax.ppermute(second, AXES, odd)
    first = lax.ppermute(first, AXES, even)
    return first, second


def fold(x):
    return jnp.sum(x.reshape(x.shape[0] // 8, 8, x.shape[1]), axis=0)


def total(x):
    return jnp.sum(x, axis=0, keepdims=True)


def in_vmem():
    return pl.BlockSpec(memory_space=pltpu.VMEM)


def pack(win, cat, cols):
    for j in range(win.shape[0] // BLOCK):
        chunk = win[j * BLOCK : (j + 1) * BLOCK, :]
        high = chunk.astype(BF16)
        cat[j * BLOCK : (j + 1) * BLOCK, :cols] = high
        cat[j * BLOCK : (j + 1) * BLOCK, cols:] = (chunk - high.astype(F32)).astype(BF16)


def load_window(meta, own, recv_e, recv_o, ext, win, cat):
    put(meta, own, recv_e, recv_o, ext)
    for j in range(win.shape[0] // BLOCK):
        win[j * BLOCK : (j + 1) * BLOCK, :] = ext[pl.ds(meta[0] + j * BLOCK, BLOCK), :]
    pack(win, cat, own.shape[1])


def multiply(a_high, a_low, cat, cols):
    wide = jnp.dot(a_high, cat[...], preferred_element_type=F32)
    narrow = jnp.dot(a_low, cat[:, :cols], preferred_element_type=F32)
    return wide[:, :cols] + (wide[:, cols:] + narrow)


def hand_out(meta, pext, p_own, p_e, p_o):
    slab, reach = p_own.shape[0], p_e.shape[0]
    right = reach + slab
    p_own[...] = pext[reach:right, :]
    p_e[...] = pext[pl.ds(pl.multiple_of(meta[1] * right, 8), reach), :]
    p_o[...] = pext[pl.ds(pl.multiple_of((1 - meta[1]) * right, 8), reach), :]


def split_kernel(block, a_high, a_low):
    rows = block.shape[1]
    at = pl.multiple_of(pl.program_id(0) * rows, rows)
    a = block[0]
    high = a.astype(BF16)
    a_high[pl.ds(at, rows), :] = high
    a_low[pl.ds(at, rows), :] = (a - high.astype(F32)).astype(BF16)


def split(schur):
    window = schur.shape[1]
    rows = BLOCK
    return pl.pallas_call(
        split_kernel,
        grid=(window // rows,),
        in_specs=[pl.BlockSpec((1, rows, window), lambda i: (0, i, 0))],
        out_specs=[in_vmem()] * 2,
        out_shape=(jax.ShapeDtypeStruct((window, window), BF16),) * 2,
        compiler_params=pltpu.CompilerParams(
            dimension_semantics=("arbitrary",), vmem_limit_bytes=8 * MIB
        ),
        cost_estimate=pl.CostEstimate(
            flops=8 * window * window * 128, bytes_accessed=8 * window * window, transcendentals=0
        ),
        name="split",
    )(pltpu.with_memory_space_constraint(schur, pltpu.HBM))


def put(meta, own, recv_e, recv_o, ext):
    slab, reach = own.shape[0], recv_e.shape[0]
    right = reach + slab
    ext[pl.ds(pl.multiple_of(meta[1] * right, 8), reach), :] = recv_e[...]
    ext[pl.ds(pl.multiple_of((1 - meta[1]) * right, 8), reach), :] = recv_o[...]
    ext[reach:right, :] = own[...]


def product_kernel(meta, a_high, a_low, own, recv_e, recv_o, *rest):
    ext, win, cat, pext = rest[-4:]
    cols = own.shape[1]
    load_window(meta, own, recv_e, recv_o, ext, win, cat)
    spread(meta, a_high, a_low, win, cat, pext, rest[:-4], cols)


def spread(meta, a_high, a_low, win, cat, pext, outs, cols):
    if len(outs) > 1:
        pext[...] = jnp.zeros(pext.shape, F32)
    else:
        outs[0][...] = jnp.zeros(outs[0].shape, F32)

    def step(j, carry):
        at = pl.multiple_of(j * BLOCK, BLOCK)
        out = multiply(a_high[pl.ds(at, BLOCK), :], a_low[pl.ds(at, BLOCK), :], cat, cols)
        if len(outs) > 1:
            pext[pl.ds(meta[0] + at, BLOCK), :] = out
        else:
            outs[0][...] += fold(win[pl.ds(at, BLOCK), :] * out)
        return carry

    lax.fori_loop(0, win.shape[0] // BLOCK, step, 0)
    if len(outs) > 1:
        hand_out(meta, pext, *outs)


def product(meta, a_high, a_low, parts, outgoing):
    slab, cols = parts[0].shape
    reach = parts[1].shape[0]
    window = a_high.shape[0]
    span = 2 * reach + slab
    vec = lambda n: jax.ShapeDtypeStruct((n, cols), F32)
    outs = (vec(slab), vec(reach), vec(reach)) if outgoing else (vec(8),)
    return pl.pallas_call(
        product_kernel,
        in_specs=[pl.BlockSpec(memory_space=pltpu.SMEM)] + [in_vmem()] * (2 + len(parts)),
        out_specs=[in_vmem()] * len(outs),
        scratch_shapes=[
            pltpu.VMEM((span, cols), F32),
            pltpu.VMEM((window, cols), F32),
            pltpu.VMEM((window, 2 * cols), BF16),
            pltpu.VMEM((span, cols), F32),
        ],
        out_shape=outs,
        compiler_params=pltpu.CompilerParams(vmem_limit_bytes=12 * MIB),
        cost_estimate=pl.CostEstimate(
            flops=8 * window * window * cols, bytes_accessed=4 * window * window, transcendentals=0
        ),
        name="product",
    )(meta, a_high, a_low, *parts)


def call(kernel, meta, args, shapes, limit=8):
    outs = tuple(jax.ShapeDtypeStruct(s, F32) for s in shapes)
    return pl.pallas_call(
        kernel,
        in_specs=[pl.BlockSpec(memory_space=pltpu.SMEM)] + [in_vmem()] * len(args),
        out_specs=[in_vmem()] * len(outs),
        out_shape=outs,
        compiler_params=pltpu.CompilerParams(vmem_limit_bytes=limit * MIB),
    )(meta, *args)


def places(meta, slab, reach):
    base = slab - reach
    even = meta[1]
    return pl.multiple_of(even * base, 8), pl.multiple_of((1 - even) * base, 8)


def gather_rows(meta, dst, p_own, recv_e, recv_o):
    slab, reach = p_own.shape[0], recv_e.shape[0]
    e_at, o_at = places(meta, slab, reach)
    dst[...] = p_own[...]
    dst[pl.ds(e_at, reach), :] += recv_e[...]
    dst[pl.ds(o_at, reach), :] += recv_o[...]


def offer(meta, src, send_e, send_o):
    slab, reach = src.shape[0], send_e.shape[0]
    e_at, o_at = places(meta, slab, reach)
    send_e[...] = src[pl.ds(e_at, reach), :]
    send_o[...] = src[pl.ds(o_at, reach), :]


def begin_kernel(meta, basis, send_e, send_o, keep, give):
    n = basis.shape[1]
    offer(meta, basis, send_e, send_o)
    gram = dot_t(basis[...], basis[...])
    share(meta, gram[: n // 2, :], gram[n // 2 :, :], keep, give)


def inverse_kernel(meta, mine, other, load, inv, y):
    n = inv.shape[0]
    inv[: n // 2, :], inv[n // 2 :, :] = shared(meta, mine[...], other[...])
    lane = lax.broadcasted_iota(jnp.int32, (1, n), 1)
    lanes = lax.broadcasted_iota(jnp.int32, (n, n), 1)

    def pick(row, k):
        return jnp.sum(jnp.where(lane == k, row, 0.0), axis=1, keepdims=True)

    def step(j, carry):
        k = 2 * j
        m = inv[...]
        col_a = jnp.sum(jnp.where(lanes == k, m, 0.0), axis=1, keepdims=True)
        col_b = jnp.sum(jnp.where(lanes == k + 1, m, 0.0), axis=1, keepdims=True)
        row_a = inv[pl.ds(k, 1), :]
        row_b = inv[pl.ds(k + 1, 1), :]
        a, b, d = pick(row_a, k), pick(row_a, k + 1), pick(row_b, k + 1)
        schur = d - b * (b / a)
        row_a = jnp.where(lane == k, 1.0, jnp.where(lane == k + 1, 0.0, row_a))
        row_b = jnp.where(lane == k, 0.0, jnp.where(lane == k + 1, 1.0, row_b))
        new_b = (row_b - (b / a) * row_a) / schur
        new_a = (row_a - b * new_b) / a
        m = jnp.where((lanes == k) | (lanes == k + 1), 0.0, m)
        inv[...] = m - col_a * new_a - col_b * new_b
        inv[pl.ds(k, 1), :] = new_a
        inv[pl.ds(k + 1, 1), :] = new_b
        return carry

    lax.fori_loop(0, n // 2, step, 0)
    y[...] = dot(inv[...], load[...])


def start_kernel(meta, p_own, recv_e, recv_o, rhs, y, c, r, send_e, send_o):
    gather_rows(meta, c, p_own, recv_e, recv_o)
    r[...] = rhs[...] - dot(c[...], y[...])
    offer(meta, r, send_e, send_o)


def share(meta, first, second, keep, give):
    n = first.shape[0]
    even = meta[1] == 1
    keep[:n, :] = jnp.where(even, first, second)
    give[:n, :] = jnp.where(even, second, first)


def shared(meta, mine, other):
    even = meta[1] == 1
    return jnp.where(even, mine, other), jnp.where(even, other, mine)


def pair_rows(meta, scalars, keep, give, n):
    even = meta[1] == 1
    keep[n:, :] = jnp.zeros((8, keep.shape[1]), F32)
    give[n:, :] = jnp.zeros((8, give.shape[1]), F32)
    for i, row in enumerate(scalars):
        keep[n + i : n + i + 1, :] = jnp.where(even, row, 0.0)
        give[n + i : n + i + 1, :] = jnp.where(even, 0.0, row)


def coarse_kernel(meta, basis, rhs, c, keep, give):
    share(meta, dot_t(basis[...], c[...]), dot_t(basis[...], rhs[...]), keep, give)


def amp_kernel(meta, mine, other, inverse, y, m, rho, amp):
    m_sum, b_sum = shared(meta, mine[...], other[...])
    coarse = b_sum - dot(m_sum, y[...])
    m[...] = m_sum
    rho[...] = coarse
    amp[...] = dot(inverse[...], coarse)


def image_kernel(meta, p_own, recv_e, recv_o, c, amp, w, send_e, send_o):
    gather_rows(meta, w, p_own, recv_e, recv_o)
    w[...] = w[...] - dot(c[...], amp[...])
    offer(meta, w, send_e, send_o)


def sums_kernel(meta, c, r, y, basis, amp, w, u, keep, give, lam):
    n = basis.shape[1]
    lam[...] = dot(basis[...], y[...])
    u[...] = r[...] - dot(basis[...], amp[...])
    share(meta, dot_t(c[...], u[...]), dot_t(c[...], w[...]), keep, give)
    pair_rows(meta, [total(u[...] * u[...]), total(u[...] * w[...])], keep, give, n)


def amp0_kernel(meta, mine, other, inverse, m, k0, a0, cq0, scal):
    n = inverse.shape[0]
    first, second = shared(meta, mine[...], other[...])
    amp = dot(inverse[...], first[:n, :])
    k0[...] = first[:n, :]
    a0[...] = amp
    cq0[...] = second[:n, :] - dot(m[...], amp)
    scal[...] = first[n:, :]


def first_kernel(meta, p_own, recv_e, recv_o, c, a0, scal, w, w1, send_e, send_o):
    gather_rows(meta, w1, p_own, recv_e, recv_o)
    alpha = scal[0:1, :] / scal[1:2, :]
    w1[...] = w[...] - alpha * (w1[...] - dot(c[...], a0[...]))
    offer(meta, w1, send_e, send_o)


def sums1_kernel(meta, basis, c, a0, k0, scal, u, w, lam, rho, p_own, recv_e, recv_o, w1,
                 lam1, u1, q0, rho1, keep, give, n0):
    n = basis.shape[1]
    gather_rows(meta, n0, p_own, recv_e, recv_o)
    alpha = scal[0:1, :] / scal[1:2, :]
    n0[...] = n0[...] - dot(c[...], a0[...])
    q0[...] = w[...] - dot(basis[...], a0[...])
    u1[...] = u[...] - alpha * q0[...]
    lam1[...] = lam[...] + alpha * u[...]
    rho1[...] = rho[...] - alpha * k0[...]
    share(meta, dot_t(c[...], u1[...]), dot_t(c[...], w1[...]), keep, give)
    pairs = ((u1, u1), (u1, w1), (u1, q0), (w1, w1), (w1, q0), (q0, q0), (n0, w1), (n0, q0))
    pair_rows(meta, [total(a[...] * b[...]) for a, b in pairs], keep, give, n)


def last_kernel(meta, mine, other, inverse, m, basis, u0, w1, u1, q0, lam1, rho1, k0, cq0, scal, lam, amp):
    n = inverse.shape[0]
    omega = total(mine[n + 8 :, :])
    first, second = shared(meta, mine[...], other[...])
    k1, l1 = first[:n, :], second[:n, :]
    uu, uw, uq, ww, wq, qq, nw, nq = (first[n + i : n + i + 1, :] for i in range(8))
    a1 = dot(inverse[...], k1)
    ma1 = dot(m[...], a1)
    beta = uu / scal[0:1, :]
    curve = uw + beta * (2.0 * uq + beta * scal[1:2, :])
    alpha = uu / curve
    mw = ww - total(a1 * k1)
    u_q1 = uw + beta * uq
    q1_q1 = mw + beta * (2.0 * wq + beta * qq)
    q1_w1 = mw + beta * wq
    m_n = nw - total(a1 * cq0[...])
    m_fm = omega + total(a1 * (ma1 - 2.0 * l1))
    q1_fq1 = m_fm + beta * (2.0 * m_n + beta * nq)
    gamma2 = uu + alpha * (alpha * q1_q1 - 2.0 * u_q1)
    delta2 = uw + alpha * (alpha * q1_fq1 - 2.0 * q1_w1)
    eps2 = u_q1 - alpha * q1_q1
    beta2 = gamma2 / uu
    p1 = u1[...] + beta * u0[...]
    q1 = w1[...] - dot(basis[...], a1) + beta * q0[...]
    curve2 = delta2 + beta2 * (2.0 * eps2 + beta2 * curve)
    alpha2 = gamma2 / curve2
    lam[...] = lam1[...] + alpha * p1 + alpha2 * (u1[...] - alpha * q1 + beta2 * p1)
    kk1 = k1 + beta * k0[...]
    k2 = k1 - alpha * (l1 - ma1 + beta * cq0[...])
    amp[...] = dot(inverse[...], rho1[...] - alpha * kk1 - alpha2 * (k2 + beta2 * kk1))


def steps(schur, offsets, rhs, basis, load):
    slab, cols = rhs.shape
    nc = basis.shape[1]
    reach = 3 * slab // 4
    index = lax.axis_index(AXES)
    meta = jnp.stack([offsets[0] - (slab - reach), 1 - index % 2]).astype(jnp.int32)
    vec, hal, sml = (slab, cols), (reach, cols), (nc, cols)
    rows8 = (8, cols)
    half = (nc + 8, cols)

    send_e, send_o, keep, give = call(
        begin_kernel, meta, (basis,), (hal, hal, (nc // 2, nc), (nc // 2, nc)))
    recv = swap(send_e, send_o)
    mine = near_sum(keep + core_swap(give))
    a_high, a_low = split(schur)
    mine = far_sum(mine)
    p_own, p_e, p_o = product(meta, a_high, a_low, (basis, *recv), True)
    recv = swap(p_e, p_o)
    other = core_swap(mine)
    inverse, y = call(inverse_kernel, meta, (mine, other, load), ((nc, nc), sml))
    c, r0, send_e, send_o = call(
        start_kernel, meta, (p_own, *recv, rhs, y), (vec, vec, hal, hal))
    recv = swap(send_e, send_o)
    keep, give = call(coarse_kernel, meta, (basis, rhs, c), (sml, sml))
    mine = near_sum(keep + core_swap(give))
    p_own, p_e, p_o = product(meta, a_high, a_low, (r0, *recv), True)
    recv = swap(p_e, p_o)
    mine = far_sum(mine)
    other = core_swap(mine)
    m, rho0, amp = call(amp_kernel, meta, (mine, other, inverse, y), (sml, sml, sml))
    w0, send_e, send_o = call(
        image_kernel, meta, (p_own, *recv, c, amp), (vec, hal, hal))
    recv = swap(send_e, send_o)
    u0, keep, give, lam0 = call(
        sums_kernel, meta, (c, r0, y, basis, amp, w0), (vec, half, half, vec))
    mine = near_sum(keep + core_swap(give))
    p_own, p_e, p_o = product(meta, a_high, a_low, (w0, *recv), True)
    recv = swap(p_e, p_o)
    mine = far_sum(mine)
    other = core_swap(mine)
    k0, a0, cq0, scal = call(
        amp0_kernel, meta, (mine, other, inverse, m), (sml, sml, sml, rows8))
    w1, send_e, send_o = call(
        first_kernel, meta, (p_own, *recv, c, a0, scal, w0), (vec, hal, hal))
    recv_in = swap(send_e, send_o)
    lam1, u1, q0, rho1, keep, give, _ = call(
        sums1_kernel, meta, (basis, c, a0, k0, scal, u0, w0, lam0, rho0, p_own, *recv, w1),
        (vec, vec, vec, sml, half, half, vec))
    mine = near_sum(keep + core_swap(give))
    (omega,) = product(meta, a_high, a_low, (w1, *recv_in), False)
    omega = near_sum(core_sum(omega))
    mine = far_sum(jnp.concatenate([mine, omega], axis=0))
    other = core_swap(mine)
    lam, amp = call(
        last_kernel, meta,
        (mine, other, inverse, m, basis, u0, w1, u1, q0, lam1, rho1, k0, cq0, scal),
        (vec, sml))
    return lam, amp


def solution(mesh):
    in_specs = (P(AXES, None, None), P(AXES), P(AXES, None), P(AXES, None), P())
    out_specs = (P(AXES, None), P())
    return jax.shard_map(steps, mesh=mesh, in_specs=in_specs, out_specs=out_specs, check_vma=False)
```

time: 1060 us -> 176 us (0.17)
  waiting for transfers between devices: 551 us -> 30.3 us
  blocking collectives: 239 us -> 0 us
  matrix products: 103 us -> 0 us
  Pallas kernels: 0 us -> 61.2 us
  other arithmetic: 34 us -> 0.28 us
  local copies, waits for them, and re-layouts: 26.2 us -> 1.06 us
  between operations: 15.5 us -> 1.74 us
    psum x5 -> x0, waiting for transfers between devices: 534 us -> none  [the longest x4 408 us: project_sum(): lax.psum((local_coarse, jnp.sum(residual * residual, axis=0)), ('gx', 'gy'))]
    psum x5 -> x0, blocking collectives: 239 us -> none  [the longest x3 134 us: project_sum(): lax.psum((local_coarse, jnp.sum(residual * residual, axis=0)), ('gx', 'gy'))]
    dot_general x13 -> x0, matrix products: 96.5 us -> none  [the longest x4 83.5 us: apply_local(): jnp.dot(schur_block, window, precision=HIGHEST, preferred_element_type=jn...]
    pallas_call x0 -> x16, Pallas kernels: none -> 61.2 us  [the longest x4 27.2 us: product(): pl.pallas_call(product_kernel, in_specs=[pl.BlockSpec(memory_space=pltpu....]
    another operation x5 -> x1, other arithmetic: 22.9 us -> 0.08 us  [steps(): jnp.stack([offsets[0] - (slab - reach), 1 - index % 2]).astype(jnp.int32)]
    dynamic_update_slice x4 -> x0, local copies, waits for them, and re-layouts: 18.3 us -> none  [apply_local(): lax.dynamic_update_slice_in_dim(spread, product_block, start_row, 0)]
    ppermute x16 -> x50, waiting for transfers between devices: 16.5 us -> 30.3 us  [the longest x28 22.6 us: exchange_sum(): out = out + lax.ppermute(value, AXES, [(j, j ^ mask) for j in range(count)])]
    ppermute x16 -> x50, starting transfers between devices: 82.9 us -> 80.8 us  [the longest x28 56.3 us: exchange_sum(): out = out + lax.ppermute(value, AXES, [(j, j ^ mask) for j in range(count)])]
  transfers between devices with their start and end apart: 21 -> 50, of which waited for: 15 -> 20; matrix products, arithmetic and copies ran while one was open for 0% -> 0% of each run, Pallas kernels for 0% -> 31%
where the time goes in v2:
time: 176 us; the launch traced here: 175 us
  starting transfers between devices  80.8 us (46%)
  Pallas kernels  61.2 us (35%)
  waiting for transfers between devices  30.3 us (17%)
    ppermute x28, starting transfers between devices, exchange_sum(): out = out + lax.ppermute(value, AXES, [(j, j ^ mask) for j in range(count)])  56.3 us
    pallas_call x4, Pallas kernels, product(): pl.pallas_call(product_kernel, in_specs=[pl.BlockSpec(memory_space=pltpu....  27.2 us
    pallas_call x11, Pallas kernels, call(): pl.pallas_call(kernel, in_specs=[pl.BlockSpec(memory_space=pltpu.SMEM)] +...  25.3 us
    ppermute x28, waiting for transfers between devices, exchange_sum(): out = out + lax.ppermute(value, AXES, [(j, j ^ mask) for j in range(count)])  22.6 us
    ppermute x7, starting transfers between devices, swap(): first = lax.ppermute(first, AXES, even)  10.1 us
    ppermute x8, starting transfers between devices, core_swap(): return lax.ppermute(value, AXES, [(i, i ^ 1) for i in range(count)])  9.51 us
    pallas_call x1, Pallas kernels, split(): pl.pallas_call(split_kernel, grid=(window // rows,), in_specs=[pl.BlockSp...  8.65 us
    ppermute x8, waiting for transfers between devices, core_swap(): return lax.ppermute(value, AXES, [(i, i ^ 1) for i in range(count)])  7.65 us
  transfers between devices with their start and end apart: 50, of which 20 were waited for; matrix products, arithmetic and copies ran while one was open for 0% of the time, Pallas kernels for 31%

profile of v2, /device:TPU:0, one launch (start us, length us, event | category | flops | bytes accessed | tf_op | source)
XLA Modules:
  0.0 175.4 jit_solution(15894735428578502498)
XLA Ops:
  4.9 4.0 %collective-permute-start.4 = (f32[64,128]{1,0:T(8,128)S(1)}, f32[64,128]{1,0:T(8,128)S(1)}, u32[]{:S(2)}, u32[]{:S(2)}) collective-permute-start(f32[64,128]{1,0:T(8,128)S(1)} %get-tuple-element.56), channel_id=1, source_target_pairs={{0,1},{1,0},{2,3},{3,2},{4,5},{5,4},{6,7},{7,6},{8,9},{9,8},{10,11... | collective-permute-start | bytes 98312 | tf_op jit(solution)/shard_map/ppermute | solution.py:49
  8.9 8.6 %split.1 = (bf16[2048,2048]{1,0:T(8,128)(2,1)S(1)}, bf16[2048,2048]{1,0:T(8,128)(2,1)S(1)}) custom-call(f32[1,2048,2048]{2,1,0:T(8,128)} %block.1), custom_call_target="tpu_custom_call" | custom-call | flops 4294967296 | bytes 33554432 | tf_op jit(solution)/shard_map/split/pallas_call | solution.py:128
  17.5 3.2 %collective-permute-start.7 = (f32[64,128]{1,0:T(8,128)S(1)}, f32[64,128]{1,0:T(8,128)S(1)}, u32[]{:S(2)}, u32[]{:S(2)}) collective-permute-start(f32[64,128]{1,0:T(8,128)S(1)} %add.107), channel_id=1, source_target_pairs={{0,6},{1,7},{2,4},{3,5},{4,2},{5,3},{6,0},{7,1},{8,14},{9,15},{10,... | collective-permute-start | bytes 98312 | tf_op jit(solution)/shard_map/ppermute | solution.py:34
  22.0 6.8 %product.4 = (f32[1024,128]{1,0:T(8,128)S(1)}, f32[768,128]{1,0:T(8,128)S(1)}, f32[768,128]{1,0:T(8,128)S(1)}) custom-call(s32[2]{0:T(128)S(1)} %pad_add_fusion.meta, bf16[2048,2048]{1,0:T(8,128)(2,1)S(1)} %get-tuple-element.48.a_high, bf16[2048,2048]{1,0:T(8,128)(2,1)S(1)} %get-tuple-element.49.a_low, f32[1024,128]{1,0:T(8,128)S(1)} %copy-done.1, ...), custom_call_target="tpu_custom_call" | custom-call | flops 4294967296 | bytes 16777216 | tf_op jit(solution)/shard_map/product/pallas_call | solution.py:186
  29.7 7.0 %collective-permute-start.10 = (f32[64,128]{1,0:T(8,128)S(1)}, f32[64,128]{1,0:T(8,128)S(1)}, u32[]{:S(2)}, u32[]{:S(2)}) collective-permute-start(f32[64,128]{1,0:T(8,128)S(1)} %add_add_fusion.7), channel_id=1, source_target_pairs={{0,24},{1,25},{2,26},{3,27},{4,28},{5,29},{6,30},{7,31},{8,16},{9,... | collective-permute-start | bytes 98312 | tf_op jit(solution)/shard_map/ppermute | solution.py:34
  38.6 2.0 %collective-permute-done.9 = f32[64,128]{1,0:T(8,128)S(1)} collective-permute-done((f32[64,128]{1,0:T(8,128)S(1)}, f32[64,128]{1,0:T(8,128)S(1)}, u32[]{:S(2)}, u32[]{:S(2)}) %collective-permute-start.9) | collective-permute-done | bytes 32800 | tf_op jit(solution)/shard_map/ppermute | solution.py:34
  42.7 8.4 %shard_map.69 = (f32[128,128]{1,0:T(8,128)S(1)}, f32[128,128]{1,0:T(8,128)S(1)}) custom-call(s32[2]{0:T(128)S(1)} %pad_add_fusion.meta, f32[64,128]{1,0:T(8,128)S(1)} %add_add_fusion.6.mine, f32[64,128]{1,0:T(8,128)S(1)} %collective-permute-done.11.other, f32[128,128]{1,0:T(8,128)S(1)} %copy-done.3), custom_call_target="tpu_custom_call" | custom-call | tf_op jit(solution)/shard_map/pallas_call | solution.py:207
  53.4 1.6 shard_map.71
  55.0 2.0 %collective-permute-start.12 = (f32[128,128]{1,0:T(8,128)S(1)}, f32[128,128]{1,0:T(8,128)S(1)}, u32[]{:S(2)}, u32[]{:S(2)}) collective-permute-start(f32[128,128]{1,0:T(8,128)S(1)} %get-tuple-element.61), channel_id=1, source_target_pairs={{0,1},{1,0},{2,3},{3,2},{4,5},{5,4},{6,7},{7,6},{8,9},{9,8},{10,11... | collective-permute-start | bytes 196616 | tf_op jit(solution)/shard_map/ppermute | solution.py:49
  57.9 3.7 %collective-permute-start.15 = (f32[128,128]{1,0:T(8,128)S(1)}, f32[128,128]{1,0:T(8,128)S(1)}, u32[]{:S(2)}, u32[]{:S(2)}) collective-permute-start(f32[128,128]{1,0:T(8,128)S(1)} %add.114), channel_id=1, source_target_pairs={{0,6},{1,7},{2,4},{3,5},{4,2},{5,3},{6,0},{7,1},{8,14},{9,15},{10,... | collective-permute-start | bytes 196616 | tf_op jit(solution)/shard_map/ppermute | solution.py:34
  62.4 6.8 %product.5 = (f32[1024,128]{1,0:T(8,128)S(1)}, f32[768,128]{1,0:T(8,128)S(1)}, f32[768,128]{1,0:T(8,128)S(1)}) custom-call(s32[2]{0:T(128)S(1)} %pad_add_fusion.meta, bf16[2048,2048]{1,0:T(8,128)(2,1)S(1)} %get-tuple-element.48.a_high, bf16[2048,2048]{1,0:T(8,128)(2,1)S(1)} %get-tuple-element.49.a_low, f32[1024,128]{1,0:T(8,128)S(1)} %get-tuple-element.59.own.r, ...), custom_call_target="tpu_custom_call" | custom-call | flops 4294967296 | bytes 16777216 | tf_op jit(solution)/shard_map/product/pallas_call | solution.py:186
  69.2 3.4 %collective-permute-start.22 = (f32[768,128]{1,0:T(8,128)S(1)}, f32[768,128]{1,0:T(8,128)S(1)}, u32[]{:S(2)}, u32[]{:S(2)}) collective-permute-start(f32[768,128]{1,0:T(8,128)S(1)} %get-tuple-element.67), channel_id=1, source_target_pairs={{0,1},{1,0},{2,3},{3,2},{4,5},{5,4},{6,7},{7,6},{8,9},{9,8},{10,11... | collective-permute-start | bytes 1179656 | tf_op jit(solution)/shard_map/ppermute | solution.py:71
  73.3 8.1 %collective-permute-start.18 = (f32[128,128]{1,0:T(8,128)S(1)}, f32[128,128]{1,0:T(8,128)S(1)}, u32[]{:S(2)}, u32[]{:S(2)}) collective-permute-start(f32[128,128]{1,0:T(8,128)S(1)} %add_add_fusion.5), channel_id=1, source_target_pairs={{0,24},{1,25},{2,26},{3,27},{4,28},{5,29},{6,30},{7,31},{8,16},{9,... | collective-permute-start | bytes 196616 | tf_op jit(solution)/shard_map/ppermute | solution.py:34
  84.3 3.2 %collective-permute-done.17 = f32[128,128]{1,0:T(8,128)S(1)} collective-permute-done((f32[128,128]{1,0:T(8,128)S(1)}, f32[128,128]{1,0:T(8,128)S(1)}, u32[]{:S(2)}, u32[]{:S(2)}) %collective-permute-start.17) | collective-permute-done | bytes 65568 | tf_op jit(solution)/shard_map/ppermute | solution.py:34
  87.5 3.2 %collective-permute-done.16 = f32[128,128]{1,0:T(8,128)S(1)} collective-permute-done((f32[128,128]{1,0:T(8,128)S(1)}, f32[128,128]{1,0:T(8,128)S(1)}, u32[]{:S(2)}, u32[]{:S(2)}) %collective-permute-start.16) | collective-permute-done | bytes 65568 | tf_op jit(solution)/shard_map/ppermute | solution.py:34
  95.2 2.5 %shard_map.74 = (f32[1024,128]{1,0:T(8,128)S(1)}, f32[136,128]{1,0:T(8,128)S(1)}, f32[136,128]{1,0:T(8,128)S(1)}, f32[1024,128]{1,0:T(8,128)S(1)}) custom-call(s32[2]{0:T(128)S(1)} %pad_add_fusion.meta, f32[1024,128]{1,0:T(8,128)S(1)} %get-tuple-element.58.c, f32[1024,128]{1,0:T(8,128)S(1)} %get-tuple-element.59.own.r, f32[128,128]{1,0:T(8,128)S(1)} %get-tuple-element.57.y, ...), custom_call_target="tpu_custom_call" | custom-call | tf_op jit(solution)/shard_map/pallas_call | solution.py:207
  97.6 1.7 collective-permute-start.24
  101.8 1.9 %collective-permute-start.26 = (f32[136,128]{1,0:T(8,128)S(1)}, f32[136,128]{1,0:T(8,128)S(1)}, u32[]{:S(2)}, u32[]{:S(2)}) collective-permute-start(f32[136,128]{1,0:T(8,128)S(1)} %add.121), channel_id=1, source_target_pairs={{0,4},{1,5},{2,6},{3,7},{4,0},{5,1},{6,2},{7,3},{8,12},{9,13},{10,... | collective-permute-start | bytes 208904 | tf_op jit(solution)/shard_map/ppermute | solution.py:34
  104.7 6.8 %product.6 = (f32[1024,128]{1,0:T(8,128)S(1)}, f32[768,128]{1,0:T(8,128)S(1)}, f32[768,128]{1,0:T(8,128)S(1)}) custom-call(s32[2]{0:T(128)S(1)} %pad_add_fusion.meta, bf16[2048,2048]{1,0:T(8,128)(2,1)S(1)} %get-tuple-element.48.a_high, bf16[2048,2048]{1,0:T(8,128)(2,1)S(1)} %get-tuple-element.49.a_low, f32[1024,128]{1,0:T(8,128)S(1)} %get-tuple-element.69.w.own, ...), custom_call_target="tpu_custom_call" | custom-call | flops 4294967296 | bytes 16777216 | tf_op jit(solution)/shard_map/product/pallas_call | solution.py:186
  111.5 5.4 %collective-permute-start.34 = (f32[768,128]{1,0:T(8,128)S(1)}, f32[768,128]{1,0:T(8,128)S(1)}, u32[]{:S(2)}, u32[]{:S(2)}) collective-permute-start(f32[768,128]{1,0:T(8,128)S(1)} %get-tuple-element.82), channel_id=1, source_target_pairs={{0,1},{1,0},{2,3},{3,2},{4,5},{5,4},{6,7},{7,6},{8,9},{9,8},{10,11... | collective-permute-start | bytes 1179656 | tf_op jit(solution)/shard_map/ppermute | solution.py:71
  117.8 2.7 %collective-permute-start.30 = (f32[136,128]{1,0:T(8,128)S(1)}, f32[136,128]{1,0:T(8,128)S(1)}, u32[]{:S(2)}, u32[]{:S(2)}) collective-permute-start(f32[136,128]{1,0:T(8,128)S(1)} %add_add_fusion.3), channel_id=1, source_target_pairs={{0,24},{1,25},{2,26},{3,27},{4,28},{5,29},{6,30},{7,31},{8,16},{9,... | collective-permute-start | bytes 208904 | tf_op jit(solution)/shard_map/ppermute | solution.py:34
  120.5 1.9 %collective-permute-start.29 = (f32[136,128]{1,0:T(8,128)S(1)}, f32[136,128]{1,0:T(8,128)S(1)}, u32[]{:S(2)}, u32[]{:S(2)}) collective-permute-start(f32[136,128]{1,0:T(8,128)S(1)} %add_add_fusion.3), channel_id=1, source_target_pairs={{0,16},{1,17},{2,18},{3,19},{4,20},{5,21},{6,22},{7,23},{8,24},{9,... | collective-permute-start | bytes 208904 | tf_op jit(solution)/shard_map/ppermute | solution.py:34
  123.8 2.1 %collective-permute-done.30 = f32[136,128]{1,0:T(8,128)S(1)} collective-permute-done((f32[136,128]{1,0:T(8,128)S(1)}, f32[136,128]{1,0:T(8,128)S(1)}, u32[]{:S(2)}, u32[]{:S(2)}) %collective-permute-start.30) | collective-permute-done | bytes 69664 | tf_op jit(solution)/shard_map/ppermute | solution.py:34
  125.9 4.9 %collective-permute-done.28 = f32[136,128]{1,0:T(8,128)S(1)} collective-permute-done((f32[136,128]{1,0:T(8,128)S(1)}, f32[136,128]{1,0:T(8,128)S(1)}, u32[]{:S(2)}, u32[]{:S(2)}) %collective-permute-start.28) | collective-permute-done | bytes 69664 | tf_op jit(solution)/shard_map/ppermute | solution.py:34
  135.3 3.5 %shard_map.77 = (f32[1024,128]{1,0:T(8,128)S(1)}, f32[1024,128]{1,0:T(8,128)S(1)}, f32[1024,128]{1,0:T(8,128)S(1)}, f32[128,128]{1,0:T(8,128)S(1)}, f32[136,128]...) custom-call(s32[2]{0:T(128)S(1)} %pad_add_fusion.meta, f32[1024,128]{1,0:T(8,128)S(1)} %copy-done.1, ...), custom_call_target="tpu_custom_call" | custom-call | tf_op jit(solution)/shard_map/pallas_call | solution.py:207
  141.4 2.7 %collective-permute-start.39 = (f32[136,128]{1,0:T(8,128)S(1)}, f32[136,128]{1,0:T(8,128)S(1)}, u32[]{:S(2)}, u32[]{:S(2)}) collective-permute-start(f32[136,128]{1,0:T(8,128)S(1)} %add.128), channel_id=1, source_target_pairs={{0,6},{1,7},{2,4},{3,5},{4,2},{5,3},{6,0},{7,1},{8,14},{9,15},{10,... | collective-permute-start | bytes 208904 | tf_op jit(solution)/shard_map/ppermute | solution.py:34
  145.8 6.7 %product.7 = f32[8,128]{1,0:T(8,128)S(1)} custom-call(s32[2]{0:T(128)S(1)} %pad_add_fusion.meta, bf16[2048,2048]{1,0:T(8,128)(2,1)S(1)} %get-tuple-element.48.a_high, bf16[2048,2048]{1,0:T(8,128)(2,1)S(1)} %get-tuple-element.49.a_low, f32[1024,128]{1,0:T(8,128)S(1)} %get-tuple-element.84.w1.own, f32[768,128]{1,0:T(8,128)S(1)} %collective-permute-done.40.recv_e, ...), custom_call_target="tpu_custom_call" | custom-call | flops 4294967296 | bytes 16777216 | tf_op jit(solution)/shard_map/product/pallas_call | solution.py:186
  152.6 6.3 %collective-permute-start.42 = (f32[8,128]{1,0:T(8,128)S(1)}, f32[8,128]{1,0:T(8,128)S(1)}, u32[]{:S(2)}, u32[]{:S(2)}) collective-permute-start(f32[8,128]{1,0:T(8,128)S(1)} %product.7), channel_id=1, source_target_pairs={{0,1},{1,0},{2,3},{3,2},{4,5},{5,4},{6,7},{7,6},{8,9},{9,8},{10,11... | collective-permute-start | bytes 12296 | tf_op jit(solution)/shard_map/ppermute | solution.py:34
  160.0 4.2 %collective-permute-start.43 = (f32[8,128]{1,0:T(8,128)S(1)}, f32[8,128]{1,0:T(8,128)S(1)}, u32[]{:S(2)}, u32[]{:S(2)}) collective-permute-start(f32[8,128]{1,0:T(8,128)S(1)} %add.132), channel_id=1, source_target_pairs={{0,2},{1,3},{2,0},{3,1},{4,6},{5,7},{6,4},{7,5},{8,10},{9,11},{10,... | collective-permute-start | bytes 12296 | tf_op jit(solution)/shard_map/ppermute | solution.py:34
  165.9 3.4 %collective-permute-start.46 = (f32[144,128]{1,0:T(8,128)S(1)}, f32[144,128]{1,0:T(8,128)S(1)}, u32[]{:S(2)}, u32[]{:S(2)}) collective-permute-start(f32[144,128]{1,0:T(8,128)S(1)} %pad_maximum_fusion), channel_id=1, source_target_pairs={{0,8},{1,9},{2,10},{3,11},{4,12},{5,13},{6,14},{7,15},{8,0},{9,1},... | collective-permute-start | bytes 221192 | tf_op jit(solution)/shard_map/ppermute | solution.py:34
  169.3 1.8 %collective-permute-done.48 = f32[144,128]{1,0:T(8,128)S(1)} collective-permute-done((f32[144,128]{1,0:T(8,128)S(1)}, f32[144,128]{1,0:T(8,128)S(1)}, u32[]{:S(2)}, u32[]{:S(2)}) %collective-permute-start.48) | collective-permute-done | bytes 73760 | tf_op jit(solution)/shard_map/ppermute | solution.py:34
  173.0 2.4 %shard_map.78 = (f32[1024,128]{1,0:T(8,128)}, f32[128,128]{1,0:T(8,128)}) custom-call(s32[2]{0:T(128)S(1)} %pad_add_fusion.meta, f32[144,128]{1,0:T(8,128)S(1)} %add_add_fusion.mine, f32[144,128]{1,0:T(8,128)S(1)} %collective-permute-done.49.other, f32[128,128]{1,0:T(8,128)S(1)} %get-tuple-element.62.inverse, f32[128,128]{1,0:T(8,128)S(1)} %get-tuple-element.72.m, ...), custom_call_target="tpu_custom_call" | custom-call | tf_op jit(solution)/shard_map/pallas_call | solution.py:207
  (108 shorter events, 40.8 us)
Async XLA Ops:
  3.6 18.4 %collective-permute-start = (f32[768,128]{1,0:T(8,128)S(1)}, f32[768,128]{1,0:T(8,128)S(1)}, u32[]{:S(2)}, u32[]{:S(2)}) collective-permute-start(f32[768,128]{1,0:T(8,128)S(1)} %get-tuple-element.50), channel_id=1, source_target_pairs={{0,1},{1,0},{2,3},{3,2},{4,5},{5,4},{6,7},{7,6},{8,9},{9,8},{10,11... | collective-permute-start | bytes 1179656 | tf_op jit(solution)/shard_map/ppermute | solution.py:71
  4.2 17.8 %collective-permute-start.1 = (f32[768,128]{1,0:T(8,128)S(1)}, f32[768,128]{1,0:T(8,128)S(1)}, u32[]{:S(2)}, u32[]{:S(2)}) collective-permute-start(f32[768,128]{1,0:T(8,128)S(1)} %get-tuple-element.51), channel_id=1, source_target_pairs={{1,2},{2,1},{3,4},{4,3},{5,6},{6,5},{7,8},{8,7},{9,10},{10,9},{11,... | collective-permute-start | bytes 1179656 | tf_op jit(solution)/shard_map/ppermute | solution.py:70
  4.9 12.6 %collective-permute-start.4 = (f32[64,128]{1,0:T(8,128)S(1)}, f32[64,128]{1,0:T(8,128)S(1)}, u32[]{:S(2)}, u32[]{:S(2)}) collective-permute-start(f32[64,128]{1,0:T(8,128)S(1)} %get-tuple-element.56), channel_id=1, source_target_pairs={{0,1},{1,0},{2,3},{3,2},{4,5},{5,4},{6,7},{7,6},{8,9},{9,8},{10,11... | collective-permute-start | bytes 98312 | tf_op jit(solution)/shard_map/ppermute | solution.py:49
  17.5 12.1 %collective-permute-start.7 = (f32[64,128]{1,0:T(8,128)S(1)}, f32[64,128]{1,0:T(8,128)S(1)}, u32[]{:S(2)}, u32[]{:S(2)}) collective-permute-start(f32[64,128]{1,0:T(8,128)S(1)} %add.107), channel_id=1, source_target_pairs={{0,6},{1,7},{2,4},{3,5},{4,2},{5,3},{6,0},{7,1},{8,14},{9,15},{10,... | collective-permute-start | bytes 98312 | tf_op jit(solution)/shard_map/ppermute | solution.py:34
  20.8 8.9 %collective-permute-start.6 = (f32[64,128]{1,0:T(8,128)S(1)}, f32[64,128]{1,0:T(8,128)S(1)}, u32[]{:S(2)}, u32[]{:S(2)}) collective-permute-start(f32[64,128]{1,0:T(8,128)S(1)} %add.107), channel_id=1, source_target_pairs={{0,4},{1,5},{2,6},{3,7},{4,0},{5,1},{6,2},{7,3},{8,12},{9,13},{10,... | collective-permute-start | bytes 98312 | tf_op jit(solution)/shard_map/ppermute | solution.py:34
  20.8 8.9 %collective-permute-start.5 = (f32[64,128]{1,0:T(8,128)S(1)}, f32[64,128]{1,0:T(8,128)S(1)}, u32[]{:S(2)}, u32[]{:S(2)}) collective-permute-start(f32[64,128]{1,0:T(8,128)S(1)} %add.107), channel_id=1, source_target_pairs={{0,2},{1,3},{2,0},{3,1},{4,6},{5,7},{6,4},{7,5},{8,10},{9,11},{10,... | collective-permute-start | bytes 98312 | tf_op jit(solution)/shard_map/ppermute | solution.py:34
  28.9 22.3 %collective-permute-start.2 = (f32[768,128]{1,0:T(8,128)S(1)}, f32[768,128]{1,0:T(8,128)S(1)}, u32[]{:S(2)}, u32[]{:S(2)}) collective-permute-start(f32[768,128]{1,0:T(8,128)S(1)} %get-tuple-element.53), channel_id=1, source_target_pairs={{0,1},{1,0},{2,3},{3,2},{4,5},{5,4},{6,7},{7,6},{8,9},{9,8},{10,11... | collective-permute-start | bytes 1179656 | tf_op jit(solution)/shard_map/ppermute | solution.py:71
  29.0 22.2 %collective-permute-start.3 = (f32[768,128]{1,0:T(8,128)S(1)}, f32[768,128]{1,0:T(8,128)S(1)}, u32[]{:S(2)}, u32[]{:S(2)}) collective-permute-start(f32[768,128]{1,0:T(8,128)S(1)} %get-tuple-element.54), channel_id=1, source_target_pairs={{1,2},{2,1},{3,4},{4,3},{5,6},{6,5},{7,8},{8,7},{9,10},{10,9},{11,... | collective-permute-start | bytes 1179656 | tf_op jit(solution)/shard_map/ppermute | solution.py:70
  29.7 8.9 %collective-permute-start.10 = (f32[64,128]{1,0:T(8,128)S(1)}, f32[64,128]{1,0:T(8,128)S(1)}, u32[]{:S(2)}, u32[]{:S(2)}) collective-permute-start(f32[64,128]{1,0:T(8,128)S(1)} %add_add_fusion.7), channel_id=1, source_target_pairs={{0,24},{1,25},{2,26},{3,27},{4,28},{5,29},{6,30},{7,31},{8,16},{9,... | collective-permute-start | bytes 98312 | tf_op jit(solution)/shard_map/ppermute | solution.py:34
  52.5 9.9 %collective-permute-start.20 = (f32[768,128]{1,0:T(8,128)S(1)}, f32[768,128]{1,0:T(8,128)S(1)}, u32[]{:S(2)}, u32[]{:S(2)}) collective-permute-start(f32[768,128]{1,0:T(8,128)S(1)} %get-tuple-element.64), channel_id=1, source_target_pairs={{0,1},{1,0},{2,3},{3,2},{4,5},{5,4},{6,7},{7,6},{8,9},{9,8},{10,11... | collective-permute-start | bytes 1179656 | tf_op jit(solution)/shard_map/ppermute | solution.py:71
  52.7 9.7 %collective-permute-start.21 = (f32[768,128]{1,0:T(8,128)S(1)}, f32[768,128]{1,0:T(8,128)S(1)}, u32[]{:S(2)}, u32[]{:S(2)}) collective-permute-start(f32[768,128]{1,0:T(8,128)S(1)} %get-tuple-element.65), channel_id=1, source_target_pairs={{1,2},{2,1},{3,4},{4,3},{5,6},{6,5},{7,8},{8,7},{9,10},{10,9},{11,... | collective-permute-start | bytes 1179656 | tf_op jit(solution)/shard_map/ppermute | solution.py:70
  57.9 15.4 %collective-permute-start.15 = (f32[128,128]{1,0:T(8,128)S(1)}, f32[128,128]{1,0:T(8,128)S(1)}, u32[]{:S(2)}, u32[]{:S(2)}) collective-permute-start(f32[128,128]{1,0:T(8,128)S(1)} %add.114), channel_id=1, source_target_pairs={{0,6},{1,7},{2,4},{3,5},{4,2},{5,3},{6,0},{7,1},{8,14},{9,15},{10,... | collective-permute-start | bytes 196616 | tf_op jit(solution)/shard_map/ppermute | solution.py:34
  61.6 11.7 %collective-permute-start.14 = (f32[128,128]{1,0:T(8,128)S(1)}, f32[128,128]{1,0:T(8,128)S(1)}, u32[]{:S(2)}, u32[]{:S(2)}) collective-permute-start(f32[128,128]{1,0:T(8,128)S(1)} %add.114), channel_id=1, source_target_pairs={{0,4},{1,5},{2,6},{3,7},{4,0},{5,1},{6,2},{7,3},{8,12},{9,13},{10,... | collective-permute-start | bytes 196616 | tf_op jit(solution)/shard_map/ppermute | solution.py:34
  61.6 11.8 %collective-permute-start.13 = (f32[128,128]{1,0:T(8,128)S(1)}, f32[128,128]{1,0:T(8,128)S(1)}, u32[]{:S(2)}, u32[]{:S(2)}) collective-permute-start(f32[128,128]{1,0:T(8,128)S(1)} %add.114), channel_id=1, source_target_pairs={{0,2},{1,3},{2,0},{3,1},{4,6},{5,7},{6,4},{7,5},{8,10},{9,11},{10,... | collective-permute-start | bytes 196616 | tf_op jit(solution)/shard_map/ppermute | solution.py:34
  69.2 23.8 %collective-permute-start.22 = (f32[768,128]{1,0:T(8,128)S(1)}, f32[768,128]{1,0:T(8,128)S(1)}, u32[]{:S(2)}, u32[]{:S(2)}) collective-permute-start(f32[768,128]{1,0:T(8,128)S(1)} %get-tuple-element.67), channel_id=1, source_target_pairs={{0,1},{1,0},{2,3},{3,2},{4,5},{5,4},{6,7},{7,6},{8,9},{9,8},{10,11... | collective-permute-start | bytes 1179656 | tf_op jit(solution)/shard_map/ppermute | solution.py:71
  72.6 20.4 %collective-permute-start.23 = (f32[768,128]{1,0:T(8,128)S(1)}, f32[768,128]{1,0:T(8,128)S(1)}, u32[]{:S(2)}, u32[]{:S(2)}) collective-permute-start(f32[768,128]{1,0:T(8,128)S(1)} %get-tuple-element.68), channel_id=1, source_target_pairs={{1,2},{2,1},{3,4},{4,3},{5,6},{6,5},{7,8},{8,7},{9,10},{10,9},{11,... | collective-permute-start | bytes 1179656 | tf_op jit(solution)/shard_map/ppermute | solution.py:70
  73.3 10.9 %collective-permute-start.18 = (f32[128,128]{1,0:T(8,128)S(1)}, f32[128,128]{1,0:T(8,128)S(1)}, u32[]{:S(2)}, u32[]{:S(2)}) collective-permute-start(f32[128,128]{1,0:T(8,128)S(1)} %add_add_fusion.5), channel_id=1, source_target_pairs={{0,24},{1,25},{2,26},{3,27},{4,28},{5,29},{6,30},{7,31},{8,16},{9,... | collective-permute-start | bytes 196616 | tf_op jit(solution)/shard_map/ppermute | solution.py:34
  81.8 8.9 %collective-permute-start.16 = (f32[128,128]{1,0:T(8,128)S(1)}, f32[128,128]{1,0:T(8,128)S(1)}, u32[]{:S(2)}, u32[]{:S(2)}) collective-permute-start(f32[128,128]{1,0:T(8,128)S(1)} %add_add_fusion.5), channel_id=1, source_target_pairs={{0,8},{1,9},{2,10},{3,11},{4,12},{5,13},{6,14},{7,15},{8,0},{9,1},... | collective-permute-start | bytes 196616 | tf_op jit(solution)/shard_map/ppermute | solution.py:34
  94.3 10.4 %collective-permute-start.32 = (f32[768,128]{1,0:T(8,128)S(1)}, f32[768,128]{1,0:T(8,128)S(1)}, u32[]{:S(2)}, u32[]{:S(2)}) collective-permute-start(f32[768,128]{1,0:T(8,128)S(1)} %get-tuple-element.79), channel_id=1, source_target_pairs={{0,1},{1,0},{2,3},{3,2},{4,5},{5,4},{6,7},{7,6},{8,9},{9,8},{10,11... | collective-permute-start | bytes 1179656 | tf_op jit(solution)/shard_map/ppermute | solution.py:71
  94.5 10.2 %collective-permute-start.33 = (f32[768,128]{1,0:T(8,128)S(1)}, f32[768,128]{1,0:T(8,128)S(1)}, u32[]{:S(2)}, u32[]{:S(2)}) collective-permute-start(f32[768,128]{1,0:T(8,128)S(1)} %get-tuple-element.80), channel_id=1, source_target_pairs={{1,2},{2,1},{3,4},{4,3},{5,6},{6,5},{7,8},{8,7},{9,10},{10,9},{11,... | collective-permute-start | bytes 1179656 | tf_op jit(solution)/shard_map/ppermute | solution.py:70
  100.2 17.5 %collective-permute-start.27 = (f32[136,128]{1,0:T(8,128)S(1)}, f32[136,128]{1,0:T(8,128)S(1)}, u32[]{:S(2)}, u32[]{:S(2)}) collective-permute-start(f32[136,128]{1,0:T(8,128)S(1)} %add.121), channel_id=1, source_target_pairs={{0,6},{1,7},{2,4},{3,5},{4,2},{5,3},{6,0},{7,1},{8,14},{9,15},{10,... | collective-permute-start | bytes 208904 | tf_op jit(solution)/shard_map/ppermute | solution.py:34
  101.8 16.0 %collective-permute-start.26 = (f32[136,128]{1,0:T(8,128)S(1)}, f32[136,128]{1,0:T(8,128)S(1)}, u32[]{:S(2)}, u32[]{:S(2)}) collective-permute-start(f32[136,128]{1,0:T(8,128)S(1)} %add.121), channel_id=1, source_target_pairs={{0,4},{1,5},{2,6},{3,7},{4,0},{5,1},{6,2},{7,3},{8,12},{9,13},{10,... | collective-permute-start | bytes 208904 | tf_op jit(solution)/shard_map/ppermute | solution.py:34
  103.7 14.1 %collective-permute-start.25 = (f32[136,128]{1,0:T(8,128)S(1)}, f32[136,128]{1,0:T(8,128)S(1)}, u32[]{:S(2)}, u32[]{:S(2)}) collective-permute-start(f32[136,128]{1,0:T(8,128)S(1)} %add.121), channel_id=1, source_target_pairs={{0,2},{1,3},{2,0},{3,1},{4,6},{5,7},{6,4},{7,5},{8,10},{9,11},{10,... | collective-permute-start | bytes 208904 | tf_op jit(solution)/shard_map/ppermute | solution.py:34
  111.5 21.7 %collective-permute-start.34 = (f32[768,128]{1,0:T(8,128)S(1)}, f32[768,128]{1,0:T(8,128)S(1)}, u32[]{:S(2)}, u32[]{:S(2)}) collective-permute-start(f32[768,128]{1,0:T(8,128)S(1)} %get-tuple-element.82), channel_id=1, source_target_pairs={{0,1},{1,0},{2,3},{3,2},{4,5},{5,4},{6,7},{7,6},{8,9},{9,8},{10,11... | collective-permute-start | bytes 1179656 | tf_op jit(solution)/shard_map/ppermute | solution.py:71
  116.9 16.3 %collective-permute-start.35 = (f32[768,128]{1,0:T(8,128)S(1)}, f32[768,128]{1,0:T(8,128)S(1)}, u32[]{:S(2)}, u32[]{:S(2)}) collective-permute-start(f32[768,128]{1,0:T(8,128)S(1)} %get-tuple-element.83), channel_id=1, source_target_pairs={{1,2},{2,1},{3,4},{4,3},{5,6},{6,5},{7,8},{8,7},{9,10},{10,9},{11,... | collective-permute-start | bytes 1179656 | tf_op jit(solution)/shard_map/ppermute | solution.py:70
  117.8 8.1 %collective-permute-start.30 = (f32[136,128]{1,0:T(8,128)S(1)}, f32[136,128]{1,0:T(8,128)S(1)}, u32[]{:S(2)}, u32[]{:S(2)}) collective-permute-start(f32[136,128]{1,0:T(8,128)S(1)} %add_add_fusion.3), channel_id=1, source_target_pairs={{0,24},{1,25},{2,26},{3,27},{4,28},{5,29},{6,30},{7,31},{8,16},{9,... | collective-permute-start | bytes 208904 | tf_op jit(solution)/shard_map/ppermute | solution.py:34
  122.4 8.4 %collective-permute-start.28 = (f32[136,128]{1,0:T(8,128)S(1)}, f32[136,128]{1,0:T(8,128)S(1)}, u32[]{:S(2)}, u32[]{:S(2)}) collective-permute-start(f32[136,128]{1,0:T(8,128)S(1)} %add_add_fusion.3), channel_id=1, source_target_pairs={{0,8},{1,9},{2,10},{3,11},{4,12},{5,13},{6,14},{7,15},{8,0},{9,1},... | collective-permute-start | bytes 208904 | tf_op jit(solution)/shard_map/ppermute | solution.py:34
  134.4 11.4 %collective-permute-start.40 = (f32[768,128]{1,0:T(8,128)S(1)}, f32[768,128]{1,0:T(8,128)S(1)}, u32[]{:S(2)}, u32[]{:S(2)}) collective-permute-start(f32[768,128]{1,0:T(8,128)S(1)} %get-tuple-element.87), channel_id=1, source_target_pairs={{0,1},{1,0},{2,3},{3,2},{4,5},{5,4},{6,7},{7,6},{8,9},{9,8},{10,11... | collective-permute-start | bytes 1179656 | tf_op jit(solution)/shard_map/ppermute | solution.py:71
  134.7 11.2 %collective-permute-start.41 = (f32[768,128]{1,0:T(8,128)S(1)}, f32[768,128]{1,0:T(8,128)S(1)}, u32[]{:S(2)}, u32[]{:S(2)}) collective-permute-start(f32[768,128]{1,0:T(8,128)S(1)} %get-tuple-element.88), channel_id=1, source_target_pairs={{1,2},{2,1},{3,4},{4,3},{5,6},{6,5},{7,8},{8,7},{9,10},{10,9},{11,... | collective-permute-start | bytes 1179656 | tf_op jit(solution)/shard_map/ppermute | solution.py:70
  141.4 18.6 %collective-permute-start.39 = (f32[136,128]{1,0:T(8,128)S(1)}, f32[136,128]{1,0:T(8,128)S(1)}, u32[]{:S(2)}, u32[]{:S(2)}) collective-permute-start(f32[136,128]{1,0:T(8,128)S(1)} %add.128), channel_id=1, source_target_pairs={{0,6},{1,7},{2,4},{3,5},{4,2},{5,3},{6,0},{7,1},{8,14},{9,15},{10,... | collective-permute-start | bytes 208904 | tf_op jit(solution)/shard_map/ppermute | solution.py:34
  144.0 20.1 %collective-permute-start.38 = (f32[136,128]{1,0:T(8,128)S(1)}, f32[136,128]{1,0:T(8,128)S(1)}, u32[]{:S(2)}, u32[]{:S(2)}) collective-permute-start(f32[136,128]{1,0:T(8,128)S(1)} %add.128), channel_id=1, source_target_pairs={{0,4},{1,5},{2,6},{3,7},{4,0},{5,1},{6,2},{7,3},{8,12},{9,13},{10,... | collective-permute-start | bytes 208904 | tf_op jit(solution)/shard_map/ppermute | solution.py:34
  144.9 19.2 %collective-permute-start.37 = (f32[136,128]{1,0:T(8,128)S(1)}, f32[136,128]{1,0:T(8,128)S(1)}, u32[]{:S(2)}, u32[]{:S(2)}) collective-permute-start(f32[136,128]{1,0:T(8,128)S(1)} %add.128), channel_id=1, source_target_pairs={{0,2},{1,3},{2,0},{3,1},{4,6},{5,7},{6,4},{7,5},{8,10},{9,11},{10,... | collective-permute-start | bytes 208904 | tf_op jit(solution)/shard_map/ppermute | solution.py:34
  (22 other events, 140.8 us)

commit v3 on v2

--- a/solution.py
+++ b/solution.py
@@ -11,6 +11,7 @@
 F32 = jnp.float32
 BF16 = jnp.bfloat16
 BLOCK = 256
+ROWS = 1024
 MIB = 1 << 20
 
 
@@ -124,7 +125,7 @@
 
 def split(schur):
     window = schur.shape[1]
-    rows = BLOCK
+    rows = 2 * BLOCK
     return pl.pallas_call(
         split_kernel,
         grid=(window // rows,),
@@ -132,7 +133,7 @@
         out_specs=[in_vmem()] * 2,
         out_shape=(jax.ShapeDtypeStruct((window, window), BF16),) * 2,
         compiler_params=pltpu.CompilerParams(
-            dimension_semantics=("arbitrary",), vmem_limit_bytes=8 * MIB
+            dimension_semantics=("arbitrary",), vmem_limit_bytes=20 * MIB
         ),
         cost_estimate=pl.CostEstimate(
             flops=8 * window * window * 128, bytes_accessed=8 * window * window, transcendentals=0
@@ -163,15 +164,15 @@
         outs[0][...] = jnp.zeros(outs[0].shape, F32)
 
     def step(j, carry):
-        at = pl.multiple_of(j * BLOCK, BLOCK)
-        out = multiply(a_high[pl.ds(at, BLOCK), :], a_low[pl.ds(at, BLOCK), :], cat, cols)
+        at = pl.multiple_of(j * ROWS, ROWS)
+        out = multiply(a_high[pl.ds(at, ROWS), :], a_low[pl.ds(at, ROWS), :], cat, cols)
         if len(outs) > 1:
-            pext[pl.ds(meta[0] + at, BLOCK), :] = out
+            pext[pl.ds(meta[0] + at, ROWS), :] = out
         else:
-            outs[0][...] += fold(win[pl.ds(at, BLOCK), :] * out)
+            outs[0][...] += fold(win[pl.ds(at, ROWS), :] * out)
         return carry
 
-    lax.fori_loop(0, win.shape[0] // BLOCK, step, 0)
+    lax.fori_loop(0, win.shape[0] // ROWS, step, 0)
     if len(outs) > 1:
         hand_out(meta, pext, *outs)
 
@@ -194,7 +195,7 @@
             pltpu.VMEM((span, cols), F32),
         ],
         out_shape=outs,
-        compiler_params=pltpu.CompilerParams(vmem_limit_bytes=12 * MIB),
+        compiler_params=pltpu.CompilerParams(vmem_limit_bytes=20 * MIB),
         cost_estimate=pl.CostEstimate(
             flops=8 * window * window * cols, bytes_accessed=4 * window * window, transcendentals=0
         ),

time: 176 us -> 169 us (0.960)
  Pallas kernels: 61.2 us -> 55.1 us
  starting transfers between devices: 80.8 us -> 79 us
    pallas_call x4, Pallas kernels: 27.2 us -> 22.5 us  [product(): pl.pallas_call(product_kernel, in_specs=[pl.BlockSpec(memory_space=pltpu....]
    ppermute x28, starting transfers between devices: 56.3 us -> 52.8 us  [exchange_sum(): out = out + lax.ppermute(value, AXES, [(j, j ^ mask) for j in range(count)])]
  transfers between devices with their start and end apart: 50 -> 50, of which waited for: 20 -> 22; matrix products, arithmetic and copies ran while one was open for 0% -> 0% of each run, Pallas kernels for 31% -> 28%
where the time goes in v3:
time: 169 us; the launch traced here: 168 us
  starting transfers between devices  79 us (47%)
  Pallas kernels  55.1 us (33%)
  waiting for transfers between devices  31.2 us (18%)
  between operations  1.72 us (1%)
    ppermute x28, starting transfers between devices, exchange_sum(): out = out + lax.ppermute(value, AXES, [(j, j ^ mask) for j in range(count)])  52.8 us
    pallas_call x11, Pallas kernels, call(): pl.pallas_call(kernel, in_specs=[pl.BlockSpec(memory_space=pltpu.SMEM)] +...  25.3 us
    ppermute x28, waiting for transfers between devices, exchange_sum(): out = out + lax.ppermute(value, AXES, [(j, j ^ mask) for j in range(count)])  23.6 us
    pallas_call x4, Pallas kernels, product(): pl.pallas_call(product_kernel, in_specs=[pl.BlockSpec(memory_space=pltpu....  22.5 us
    ppermute x7, starting transfers between devices, swap(): first = lax.ppermute(first, AXES, even)  11.8 us
    ppermute x8, starting transfers between devices, core_swap(): return lax.ppermute(value, AXES, [(i, i ^ 1) for i in range(count)])  9.48 us
    ppermute x8, waiting for transfers between devices, core_swap(): return lax.ppermute(value, AXES, [(i, i ^ 1) for i in range(count)])  7.65 us
    pallas_call x1, Pallas kernels, split(): pl.pallas_call(split_kernel, grid=(window // rows,), in_specs=[pl.BlockSp...  7.33 us
  transfers between devices with their start and end apart: 50, of which 22 were waited for; matrix products, arithmetic and copies ran while one was open for 0% of the time, Pallas kernels for 28%

profile of v3, /device:TPU:0, one launch (start us, length us, event | category | flops | bytes accessed | tf_op | source)
XLA Modules:
  0.0 168.4 jit_solution(4457466131217059267)
XLA Ops:
  4.9 4.0 %collective-permute-start.4 = (f32[64,128]{1,0:T(8,128)S(1)}, f32[64,128]{1,0:T(8,128)S(1)}, u32[]{:S(2)}, u32[]{:S(2)}) collective-permute-start(f32[64,128]{1,0:T(8,128)S(1)} %get-tuple-element.56), channel_id=1, source_target_pairs={{0,1},{1,0},{2,3},{3,2},{4,5},{5,4},{6,7},{7,6},{8,9},{9,8},{10,11... | collective-permute-start | bytes 98312 | tf_op jit(solution)/shard_map/ppermute | solution.py:50
  8.9 7.3 %split.1 = (bf16[2048,2048]{1,0:T(8,128)(2,1)S(1)}, bf16[2048,2048]{1,0:T(8,128)(2,1)S(1)}) custom-call(f32[1,2048,2048]{2,1,0:T(8,128)} %block.1), custom_call_target="tpu_custom_call" | custom-call | flops 4294967296 | bytes 33554432 | tf_op jit(solution)/shard_map/split/pallas_call | solution.py:129
  16.2 3.2 %collective-permute-start.7 = (f32[64,128]{1,0:T(8,128)S(1)}, f32[64,128]{1,0:T(8,128)S(1)}, u32[]{:S(2)}, u32[]{:S(2)}) collective-permute-start(f32[64,128]{1,0:T(8,128)S(1)} %add.107), channel_id=1, source_target_pairs={{0,6},{1,7},{2,4},{3,5},{4,2},{5,3},{6,0},{7,1},{8,14},{9,15},{10,... | collective-permute-start | bytes 98312 | tf_op jit(solution)/shard_map/ppermute | solution.py:35
  20.7 5.6 %product.4 = (f32[1024,128]{1,0:T(8,128)S(1)}, f32[768,128]{1,0:T(8,128)S(1)}, f32[768,128]{1,0:T(8,128)S(1)}) custom-call(s32[2]{0:T(128)S(1)} %pad_add_fusion.meta, bf16[2048,2048]{1,0:T(8,128)(2,1)S(1)} %get-tuple-element.48.a_high, bf16[2048,2048]{1,0:T(8,128)(2,1)S(1)} %get-tuple-element.49.a_low, f32[1024,128]{1,0:T(8,128)S(1)} %copy-done.1, ...), custom_call_target="tpu_custom_call" | custom-call | flops 4294967296 | bytes 16777216 | tf_op jit(solution)/shard_map/product/pallas_call | solution.py:187
  27.2 7.0 %collective-permute-start.10 = (f32[64,128]{1,0:T(8,128)S(1)}, f32[64,128]{1,0:T(8,128)S(1)}, u32[]{:S(2)}, u32[]{:S(2)}) collective-permute-start(f32[64,128]{1,0:T(8,128)S(1)} %add_add_fusion.7), channel_id=1, source_target_pairs={{0,24},{1,25},{2,26},{3,27},{4,28},{5,29},{6,30},{7,31},{8,16},{9,... | collective-permute-start | bytes 98312 | tf_op jit(solution)/shard_map/ppermute | solution.py:35
  36.1 2.0 %collective-permute-done.9 = f32[64,128]{1,0:T(8,128)S(1)} collective-permute-done((f32[64,128]{1,0:T(8,128)S(1)}, f32[64,128]{1,0:T(8,128)S(1)}, u32[]{:S(2)}, u32[]{:S(2)}) %collective-permute-start.9) | collective-permute-done | bytes 32800 | tf_op jit(solution)/shard_map/ppermute | solution.py:35
  40.2 8.4 %shard_map.69 = (f32[128,128]{1,0:T(8,128)S(1)}, f32[128,128]{1,0:T(8,128)S(1)}) custom-call(s32[2]{0:T(128)S(1)} %pad_add_fusion.meta, f32[64,128]{1,0:T(8,128)S(1)} %add_add_fusion.6.mine, f32[64,128]{1,0:T(8,128)S(1)} %collective-permute-done.11.other, f32[128,128]{1,0:T(8,128)S(1)} %copy-done.3), custom_call_target="tpu_custom_call" | custom-call | tf_op jit(solution)/shard_map/pallas_call | solution.py:208
  50.9 1.6 shard_map.71
  52.5 2.0 %collective-permute-start.12 = (f32[128,128]{1,0:T(8,128)S(1)}, f32[128,128]{1,0:T(8,128)S(1)}, u32[]{:S(2)}, u32[]{:S(2)}) collective-permute-start(f32[128,128]{1,0:T(8,128)S(1)} %get-tuple-element.61), channel_id=1, source_target_pairs={{0,1},{1,0},{2,3},{3,2},{4,5},{5,4},{6,7},{7,6},{8,9},{9,8},{10,11... | collective-permute-start | bytes 196616 | tf_op jit(solution)/shard_map/ppermute | solution.py:50
  55.4 3.7 %collective-permute-start.15 = (f32[128,128]{1,0:T(8,128)S(1)}, f32[128,128]{1,0:T(8,128)S(1)}, u32[]{:S(2)}, u32[]{:S(2)}) collective-permute-start(f32[128,128]{1,0:T(8,128)S(1)} %add.114), channel_id=1, source_target_pairs={{0,6},{1,7},{2,4},{3,5},{4,2},{5,3},{6,0},{7,1},{8,14},{9,15},{10,... | collective-permute-start | bytes 196616 | tf_op jit(solution)/shard_map/ppermute | solution.py:35
  59.8 5.6 %product.5 = (f32[1024,128]{1,0:T(8,128)S(1)}, f32[768,128]{1,0:T(8,128)S(1)}, f32[768,128]{1,0:T(8,128)S(1)}) custom-call(s32[2]{0:T(128)S(1)} %pad_add_fusion.meta, bf16[2048,2048]{1,0:T(8,128)(2,1)S(1)} %get-tuple-element.48.a_high, bf16[2048,2048]{1,0:T(8,128)(2,1)S(1)} %get-tuple-element.49.a_low, f32[1024,128]{1,0:T(8,128)S(1)} %get-tuple-element.59.own.r, ...), custom_call_target="tpu_custom_call" | custom-call | flops 4294967296 | bytes 16777216 | tf_op jit(solution)/shard_map/product/pallas_call | solution.py:187
  65.5 3.4 %collective-permute-start.22 = (f32[768,128]{1,0:T(8,128)S(1)}, f32[768,128]{1,0:T(8,128)S(1)}, u32[]{:S(2)}, u32[]{:S(2)}) collective-permute-start(f32[768,128]{1,0:T(8,128)S(1)} %get-tuple-element.67), channel_id=1, source_target_pairs={{0,1},{1,0},{2,3},{3,2},{4,5},{5,4},{6,7},{7,6},{8,9},{9,8},{10,11... | collective-permute-start | bytes 1179656 | tf_op jit(solution)/shard_map/ppermute | solution.py:72
  69.7 8.0 %collective-permute-start.18 = (f32[128,128]{1,0:T(8,128)S(1)}, f32[128,128]{1,0:T(8,128)S(1)}, u32[]{:S(2)}, u32[]{:S(2)}) collective-permute-start(f32[128,128]{1,0:T(8,128)S(1)} %add_add_fusion.5), channel_id=1, source_target_pairs={{0,24},{1,25},{2,26},{3,27},{4,28},{5,29},{6,30},{7,31},{8,16},{9,... | collective-permute-start | bytes 196616 | tf_op jit(solution)/shard_map/ppermute | solution.py:35
  80.6 3.2 %collective-permute-done.17 = f32[128,128]{1,0:T(8,128)S(1)} collective-permute-done((f32[128,128]{1,0:T(8,128)S(1)}, f32[128,128]{1,0:T(8,128)S(1)}, u32[]{:S(2)}, u32[]{:S(2)}) %collective-permute-start.17) | collective-permute-done | bytes 65568 | tf_op jit(solution)/shard_map/ppermute | solution.py:35
  83.8 3.2 %collective-permute-done.16 = f32[128,128]{1,0:T(8,128)S(1)} collective-permute-done((f32[128,128]{1,0:T(8,128)S(1)}, f32[128,128]{1,0:T(8,128)S(1)}, u32[]{:S(2)}, u32[]{:S(2)}) %collective-permute-start.16) | collective-permute-done | bytes 65568 | tf_op jit(solution)/shard_map/ppermute | solution.py:35
  91.7 2.5 %shard_map.74 = (f32[1024,128]{1,0:T(8,128)S(1)}, f32[136,128]{1,0:T(8,128)S(1)}, f32[136,128]{1,0:T(8,128)S(1)}, f32[1024,128]{1,0:T(8,128)S(1)}) custom-call(s32[2]{0:T(128)S(1)} %pad_add_fusion.meta, f32[1024,128]{1,0:T(8,128)S(1)} %get-tuple-element.58.c, f32[1024,128]{1,0:T(8,128)S(1)} %get-tuple-element.59.own.r, f32[128,128]{1,0:T(8,128)S(1)} %get-tuple-element.57.y, ...), custom_call_target="tpu_custom_call" | custom-call | tf_op jit(solution)/shard_map/pallas_call | solution.py:208
  94.1 1.6 collective-permute-start.24
  96.7 2.7 %collective-permute-start.27 = (f32[136,128]{1,0:T(8,128)S(1)}, f32[136,128]{1,0:T(8,128)S(1)}, u32[]{:S(2)}, u32[]{:S(2)}) collective-permute-start(f32[136,128]{1,0:T(8,128)S(1)} %add.121), channel_id=1, source_target_pairs={{0,6},{1,7},{2,4},{3,5},{4,2},{5,3},{6,0},{7,1},{8,14},{9,15},{10,... | collective-permute-start | bytes 208904 | tf_op jit(solution)/shard_map/ppermute | solution.py:35
  101.2 5.7 %product.6 = (f32[1024,128]{1,0:T(8,128)S(1)}, f32[768,128]{1,0:T(8,128)S(1)}, f32[768,128]{1,0:T(8,128)S(1)}) custom-call(s32[2]{0:T(128)S(1)} %pad_add_fusion.meta, bf16[2048,2048]{1,0:T(8,128)(2,1)S(1)} %get-tuple-element.48.a_high, bf16[2048,2048]{1,0:T(8,128)(2,1)S(1)} %get-tuple-element.49.a_low, f32[1024,128]{1,0:T(8,128)S(1)} %get-tuple-element.69.w.own, ...), custom_call_target="tpu_custom_call" | custom-call | flops 4294967296 | bytes 16777216 | tf_op jit(solution)/shard_map/product/pallas_call | solution.py:187
  106.8 7.2 %collective-permute-start.34 = (f32[768,128]{1,0:T(8,128)S(1)}, f32[768,128]{1,0:T(8,128)S(1)}, u32[]{:S(2)}, u32[]{:S(2)}) collective-permute-start(f32[768,128]{1,0:T(8,128)S(1)} %get-tuple-element.82), channel_id=1, source_target_pairs={{0,1},{1,0},{2,3},{3,2},{4,5},{5,4},{6,7},{7,6},{8,9},{9,8},{10,11... | collective-permute-start | bytes 1179656 | tf_op jit(solution)/shard_map/ppermute | solution.py:72
  115.6 1.5 collective-permute-start.29
  118.5 2.1 %collective-permute-done.30 = f32[136,128]{1,0:T(8,128)S(1)} collective-permute-done((f32[136,128]{1,0:T(8,128)S(1)}, f32[136,128]{1,0:T(8,128)S(1)}, u32[]{:S(2)}, u32[]{:S(2)}) %collective-permute-start.30) | collective-permute-done | bytes 69664 | tf_op jit(solution)/shard_map/ppermute | solution.py:35
  121.7 4.6 %collective-permute-done.28 = f32[136,128]{1,0:T(8,128)S(1)} collective-permute-done((f32[136,128]{1,0:T(8,128)S(1)}, f32[136,128]{1,0:T(8,128)S(1)}, u32[]{:S(2)}, u32[]{:S(2)}) %collective-permute-start.28) | collective-permute-done | bytes 69664 | tf_op jit(solution)/shard_map/ppermute | solution.py:35
  130.8 3.5 %shard_map.77 = (f32[1024,128]{1,0:T(8,128)S(1)}, f32[1024,128]{1,0:T(8,128)S(1)}, f32[1024,128]{1,0:T(8,128)S(1)}, f32[128,128]{1,0:T(8,128)S(1)}, f32[136,128]...) custom-call(s32[2]{0:T(128)S(1)} %pad_add_fusion.meta, f32[1024,128]{1,0:T(8,128)S(1)} %copy-done.1, ...), custom_call_target="tpu_custom_call" | custom-call | tf_op jit(solution)/shard_map/pallas_call | solution.py:208
  134.4 1.6 collective-permute-start.36
  136.9 2.6 %collective-permute-start.39 = (f32[136,128]{1,0:T(8,128)S(1)}, f32[136,128]{1,0:T(8,128)S(1)}, u32[]{:S(2)}, u32[]{:S(2)}) collective-permute-start(f32[136,128]{1,0:T(8,128)S(1)} %add.128), channel_id=1, source_target_pairs={{0,6},{1,7},{2,4},{3,5},{4,2},{5,3},{6,0},{7,1},{8,14},{9,15},{10,... | collective-permute-start | bytes 208904 | tf_op jit(solution)/shard_map/ppermute | solution.py:35
  141.3 5.5 %product.7 = f32[8,128]{1,0:T(8,128)S(1)} custom-call(s32[2]{0:T(128)S(1)} %pad_add_fusion.meta, bf16[2048,2048]{1,0:T(8,128)(2,1)S(1)} %get-tuple-element.48.a_high, bf16[2048,2048]{1,0:T(8,128)(2,1)S(1)} %get-tuple-element.49.a_low, f32[1024,128]{1,0:T(8,128)S(1)} %get-tuple-element.84.w1.own, f32[768,128]{1,0:T(8,128)S(1)} %collective-permute-done.40.recv_e, ...), custom_call_target="tpu_custom_call" | custom-call | flops 4294967296 | bytes 16777216 | tf_op jit(solution)/shard_map/product/pallas_call | solution.py:187
  146.9 5.2 %collective-permute-start.42 = (f32[8,128]{1,0:T(8,128)S(1)}, f32[8,128]{1,0:T(8,128)S(1)}, u32[]{:S(2)}, u32[]{:S(2)}) collective-permute-start(f32[8,128]{1,0:T(8,128)S(1)} %product.7), channel_id=1, source_target_pairs={{0,1},{1,0},{2,3},{3,2},{4,5},{5,4},{6,7},{7,6},{8,9},{9,8},{10,11... | collective-permute-start | bytes 12296 | tf_op jit(solution)/shard_map/ppermute | solution.py:35
  154.0 3.2 %collective-permute-start.43 = (f32[8,128]{1,0:T(8,128)S(1)}, f32[8,128]{1,0:T(8,128)S(1)}, u32[]{:S(2)}, u32[]{:S(2)}) collective-permute-start(f32[8,128]{1,0:T(8,128)S(1)} %add.132), channel_id=1, source_target_pairs={{0,2},{1,3},{2,0},{3,1},{4,6},{5,7},{6,4},{7,5},{8,10},{9,11},{10,... | collective-permute-start | bytes 12296 | tf_op jit(solution)/shard_map/ppermute | solution.py:35
  160.0 2.4 %collective-permute-start.46 = (f32[144,128]{1,0:T(8,128)S(1)}, f32[144,128]{1,0:T(8,128)S(1)}, u32[]{:S(2)}, u32[]{:S(2)}) collective-permute-start(f32[144,128]{1,0:T(8,128)S(1)} %pad_maximum_fusion), channel_id=1, source_target_pairs={{0,8},{1,9},{2,10},{3,11},{4,12},{5,13},{6,14},{7,15},{8,0},{9,1},... | collective-permute-start | bytes 221192 | tf_op jit(solution)/shard_map/ppermute | solution.py:35
  162.4 1.8 %collective-permute-done.48 = f32[144,128]{1,0:T(8,128)S(1)} collective-permute-done((f32[144,128]{1,0:T(8,128)S(1)}, f32[144,128]{1,0:T(8,128)S(1)}, u32[]{:S(2)}, u32[]{:S(2)}) %collective-permute-start.48) | collective-permute-done | bytes 73760 | tf_op jit(solution)/shard_map/ppermute | solution.py:35
  166.1 2.4 %shard_map.78 = (f32[1024,128]{1,0:T(8,128)}, f32[128,128]{1,0:T(8,128)}) custom-call(s32[2]{0:T(128)S(1)} %pad_add_fusion.meta, f32[144,128]{1,0:T(8,128)S(1)} %add_add_fusion.mine, f32[144,128]{1,0:T(8,128)S(1)} %collective-permute-done.49.other, f32[128,128]{1,0:T(8,128)S(1)} %get-tuple-element.62.inverse, f32[128,128]{1,0:T(8,128)S(1)} %get-tuple-element.72.m, ...), custom_call_target="tpu_custom_call" | custom-call | tf_op jit(solution)/shard_map/pallas_call | solution.py:208
  (108 shorter events, 42.5 us)
Async XLA Ops:
  3.6 17.1 %collective-permute-start = (f32[768,128]{1,0:T(8,128)S(1)}, f32[768,128]{1,0:T(8,128)S(1)}, u32[]{:S(2)}, u32[]{:S(2)}) collective-permute-start(f32[768,128]{1,0:T(8,128)S(1)} %get-tuple-element.50), channel_id=1, source_target_pairs={{0,1},{1,0},{2,3},{3,2},{4,5},{5,4},{6,7},{7,6},{8,9},{9,8},{10,11... | collective-permute-start | bytes 1179656 | tf_op jit(solution)/shard_map/ppermute | solution.py:72
  4.2 16.5 %collective-permute-start.1 = (f32[768,128]{1,0:T(8,128)S(1)}, f32[768,128]{1,0:T(8,128)S(1)}, u32[]{:S(2)}, u32[]{:S(2)}) collective-permute-start(f32[768,128]{1,0:T(8,128)S(1)} %get-tuple-element.51), channel_id=1, source_target_pairs={{1,2},{2,1},{3,4},{4,3},{5,6},{6,5},{7,8},{8,7},{9,10},{10,9},{11,... | collective-permute-start | bytes 1179656 | tf_op jit(solution)/shard_map/ppermute | solution.py:71
  4.9 11.3 %collective-permute-start.4 = (f32[64,128]{1,0:T(8,128)S(1)}, f32[64,128]{1,0:T(8,128)S(1)}, u32[]{:S(2)}, u32[]{:S(2)}) collective-permute-start(f32[64,128]{1,0:T(8,128)S(1)} %get-tuple-element.56), channel_id=1, source_target_pairs={{0,1},{1,0},{2,3},{3,2},{4,5},{5,4},{6,7},{7,6},{8,9},{9,8},{10,11... | collective-permute-start | bytes 98312 | tf_op jit(solution)/shard_map/ppermute | solution.py:50
  16.2 10.9 %collective-permute-start.7 = (f32[64,128]{1,0:T(8,128)S(1)}, f32[64,128]{1,0:T(8,128)S(1)}, u32[]{:S(2)}, u32[]{:S(2)}) collective-permute-start(f32[64,128]{1,0:T(8,128)S(1)} %add.107), channel_id=1, source_target_pairs={{0,6},{1,7},{2,4},{3,5},{4,2},{5,3},{6,0},{7,1},{8,14},{9,15},{10,... | collective-permute-start | bytes 98312 | tf_op jit(solution)/shard_map/ppermute | solution.py:35
  19.5 7.7 %collective-permute-start.6 = (f32[64,128]{1,0:T(8,128)S(1)}, f32[64,128]{1,0:T(8,128)S(1)}, u32[]{:S(2)}, u32[]{:S(2)}) collective-permute-start(f32[64,128]{1,0:T(8,128)S(1)} %add.107), channel_id=1, source_target_pairs={{0,4},{1,5},{2,6},{3,7},{4,0},{5,1},{6,2},{7,3},{8,12},{9,13},{10,... | collective-permute-start | bytes 98312 | tf_op jit(solution)/shard_map/ppermute | solution.py:35
  19.5 7.7 %collective-permute-start.5 = (f32[64,128]{1,0:T(8,128)S(1)}, f32[64,128]{1,0:T(8,128)S(1)}, u32[]{:S(2)}, u32[]{:S(2)}) collective-permute-start(f32[64,128]{1,0:T(8,128)S(1)} %add.107), channel_id=1, source_target_pairs={{0,2},{1,3},{2,0},{3,1},{4,6},{5,7},{6,4},{7,5},{8,10},{9,11},{10,... | collective-permute-start | bytes 98312 | tf_op jit(solution)/shard_map/ppermute | solution.py:35
  26.4 22.3 %collective-permute-start.2 = (f32[768,128]{1,0:T(8,128)S(1)}, f32[768,128]{1,0:T(8,128)S(1)}, u32[]{:S(2)}, u32[]{:S(2)}) collective-permute-start(f32[768,128]{1,0:T(8,128)S(1)} %get-tuple-element.53), channel_id=1, source_target_pairs={{0,1},{1,0},{2,3},{3,2},{4,5},{5,4},{6,7},{7,6},{8,9},{9,8},{10,11... | collective-permute-start | bytes 1179656 | tf_op jit(solution)/shard_map/ppermute | solution.py:72
  26.4 22.2 %collective-permute-start.3 = (f32[768,128]{1,0:T(8,128)S(1)}, f32[768,128]{1,0:T(8,128)S(1)}, u32[]{:S(2)}, u32[]{:S(2)}) collective-permute-start(f32[768,128]{1,0:T(8,128)S(1)} %get-tuple-element.54), channel_id=1, source_target_pairs={{1,2},{2,1},{3,4},{4,3},{5,6},{6,5},{7,8},{8,7},{9,10},{10,9},{11,... | collective-permute-start | bytes 1179656 | tf_op jit(solution)/shard_map/ppermute | solution.py:71
  27.2 8.9 %collective-permute-start.10 = (f32[64,128]{1,0:T(8,128)S(1)}, f32[64,128]{1,0:T(8,128)S(1)}, u32[]{:S(2)}, u32[]{:S(2)}) collective-permute-start(f32[64,128]{1,0:T(8,128)S(1)} %add_add_fusion.7), channel_id=1, source_target_pairs={{0,24},{1,25},{2,26},{3,27},{4,28},{5,29},{6,30},{7,31},{8,16},{9,... | collective-permute-start | bytes 98312 | tf_op jit(solution)/shard_map/ppermute | solution.py:35
  50.0 9.9 %collective-permute-start.20 = (f32[768,128]{1,0:T(8,128)S(1)}, f32[768,128]{1,0:T(8,128)S(1)}, u32[]{:S(2)}, u32[]{:S(2)}) collective-permute-start(f32[768,128]{1,0:T(8,128)S(1)} %get-tuple-element.64), channel_id=1, source_target_pairs={{0,1},{1,0},{2,3},{3,2},{4,5},{5,4},{6,7},{7,6},{8,9},{9,8},{10,11... | collective-permute-start | bytes 1179656 | tf_op jit(solution)/shard_map/ppermute | solution.py:72
  50.2 9.6 %collective-permute-start.21 = (f32[768,128]{1,0:T(8,128)S(1)}, f32[768,128]{1,0:T(8,128)S(1)}, u32[]{:S(2)}, u32[]{:S(2)}) collective-permute-start(f32[768,128]{1,0:T(8,128)S(1)} %get-tuple-element.65), channel_id=1, source_target_pairs={{1,2},{2,1},{3,4},{4,3},{5,6},{6,5},{7,8},{8,7},{9,10},{10,9},{11,... | collective-permute-start | bytes 1179656 | tf_op jit(solution)/shard_map/ppermute | solution.py:71
  55.4 14.2 %collective-permute-start.15 = (f32[128,128]{1,0:T(8,128)S(1)}, f32[128,128]{1,0:T(8,128)S(1)}, u32[]{:S(2)}, u32[]{:S(2)}) collective-permute-start(f32[128,128]{1,0:T(8,128)S(1)} %add.114), channel_id=1, source_target_pairs={{0,6},{1,7},{2,4},{3,5},{4,2},{5,3},{6,0},{7,1},{8,14},{9,15},{10,... | collective-permute-start | bytes 196616 | tf_op jit(solution)/shard_map/ppermute | solution.py:35
  59.1 10.6 %collective-permute-start.14 = (f32[128,128]{1,0:T(8,128)S(1)}, f32[128,128]{1,0:T(8,128)S(1)}, u32[]{:S(2)}, u32[]{:S(2)}) collective-permute-start(f32[128,128]{1,0:T(8,128)S(1)} %add.114), channel_id=1, source_target_pairs={{0,4},{1,5},{2,6},{3,7},{4,0},{5,1},{6,2},{7,3},{8,12},{9,13},{10,... | collective-permute-start | bytes 196616 | tf_op jit(solution)/shard_map/ppermute | solution.py:35
  59.1 10.6 %collective-permute-start.13 = (f32[128,128]{1,0:T(8,128)S(1)}, f32[128,128]{1,0:T(8,128)S(1)}, u32[]{:S(2)}, u32[]{:S(2)}) collective-permute-start(f32[128,128]{1,0:T(8,128)S(1)} %add.114), channel_id=1, source_target_pairs={{0,2},{1,3},{2,0},{3,1},{4,6},{5,7},{6,4},{7,5},{8,10},{9,11},{10,... | collective-permute-start | bytes 196616 | tf_op jit(solution)/shard_map/ppermute | solution.py:35
  65.5 23.8 %collective-permute-start.22 = (f32[768,128]{1,0:T(8,128)S(1)}, f32[768,128]{1,0:T(8,128)S(1)}, u32[]{:S(2)}, u32[]{:S(2)}) collective-permute-start(f32[768,128]{1,0:T(8,128)S(1)} %get-tuple-element.67), channel_id=1, source_target_pairs={{0,1},{1,0},{2,3},{3,2},{4,5},{5,4},{6,7},{7,6},{8,9},{9,8},{10,11... | collective-permute-start | bytes 1179656 | tf_op jit(solution)/shard_map/ppermute | solution.py:72
  68.8 20.5 %collective-permute-start.23 = (f32[768,128]{1,0:T(8,128)S(1)}, f32[768,128]{1,0:T(8,128)S(1)}, u32[]{:S(2)}, u32[]{:S(2)}) collective-permute-start(f32[768,128]{1,0:T(8,128)S(1)} %get-tuple-element.68), channel_id=1, source_target_pairs={{1,2},{2,1},{3,4},{4,3},{5,6},{6,5},{7,8},{8,7},{9,10},{10,9},{11,... | collective-permute-start | bytes 1179656 | tf_op jit(solution)/shard_map/ppermute | solution.py:71
  69.7 10.9 %collective-permute-start.18 = (f32[128,128]{1,0:T(8,128)S(1)}, f32[128,128]{1,0:T(8,128)S(1)}, u32[]{:S(2)}, u32[]{:S(2)}) collective-permute-start(f32[128,128]{1,0:T(8,128)S(1)} %add_add_fusion.5), channel_id=1, source_target_pairs={{0,24},{1,25},{2,26},{3,27},{4,28},{5,29},{6,30},{7,31},{8,16},{9,... | collective-permute-start | bytes 196616 | tf_op jit(solution)/shard_map/ppermute | solution.py:35
  78.0 8.9 %collective-permute-start.16 = (f32[128,128]{1,0:T(8,128)S(1)}, f32[128,128]{1,0:T(8,128)S(1)}, u32[]{:S(2)}, u32[]{:S(2)}) collective-permute-start(f32[128,128]{1,0:T(8,128)S(1)} %add_add_fusion.5), channel_id=1, source_target_pairs={{0,8},{1,9},{2,10},{3,11},{4,12},{5,13},{6,14},{7,15},{8,0},{9,1},... | collective-permute-start | bytes 196616 | tf_op jit(solution)/shard_map/ppermute | solution.py:35
  90.6 10.6 %collective-permute-start.32 = (f32[768,128]{1,0:T(8,128)S(1)}, f32[768,128]{1,0:T(8,128)S(1)}, u32[]{:S(2)}, u32[]{:S(2)}) collective-permute-start(f32[768,128]{1,0:T(8,128)S(1)} %get-tuple-element.79), channel_id=1, source_target_pairs={{0,1},{1,0},{2,3},{3,2},{4,5},{5,4},{6,7},{7,6},{8,9},{9,8},{10,11... | collective-permute-start | bytes 1179656 | tf_op jit(solution)/shard_map/ppermute | solution.py:72
  90.8 10.4 %collective-permute-start.33 = (f32[768,128]{1,0:T(8,128)S(1)}, f32[768,128]{1,0:T(8,128)S(1)}, u32[]{:S(2)}, u32[]{:S(2)}) collective-permute-start(f32[768,128]{1,0:T(8,128)S(1)} %get-tuple-element.80), channel_id=1, source_target_pairs={{1,2},{2,1},{3,4},{4,3},{5,6},{6,5},{7,8},{8,7},{9,10},{10,9},{11,... | collective-permute-start | bytes 1179656 | tf_op jit(solution)/shard_map/ppermute | solution.py:71
  96.7 18.0 %collective-permute-start.27 = (f32[136,128]{1,0:T(8,128)S(1)}, f32[136,128]{1,0:T(8,128)S(1)}, u32[]{:S(2)}, u32[]{:S(2)}) collective-permute-start(f32[136,128]{1,0:T(8,128)S(1)} %add.121), channel_id=1, source_target_pairs={{0,6},{1,7},{2,4},{3,5},{4,2},{5,3},{6,0},{7,1},{8,14},{9,15},{10,... | collective-permute-start | bytes 208904 | tf_op jit(solution)/shard_map/ppermute | solution.py:35
  99.4 15.3 %collective-permute-start.26 = (f32[136,128]{1,0:T(8,128)S(1)}, f32[136,128]{1,0:T(8,128)S(1)}, u32[]{:S(2)}, u32[]{:S(2)}) collective-permute-start(f32[136,128]{1,0:T(8,128)S(1)} %add.121), channel_id=1, source_target_pairs={{0,4},{1,5},{2,6},{3,7},{4,0},{5,1},{6,2},{7,3},{8,12},{9,13},{10,... | collective-permute-start | bytes 208904 | tf_op jit(solution)/shard_map/ppermute | solution.py:35
  100.2 14.5 %collective-permute-start.25 = (f32[136,128]{1,0:T(8,128)S(1)}, f32[136,128]{1,0:T(8,128)S(1)}, u32[]{:S(2)}, u32[]{:S(2)}) collective-permute-start(f32[136,128]{1,0:T(8,128)S(1)} %add.121), channel_id=1, source_target_pairs={{0,2},{1,3},{2,0},{3,1},{4,6},{5,7},{6,4},{7,5},{8,10},{9,11},{10,... | collective-permute-start | bytes 208904 | tf_op jit(solution)/shard_map/ppermute | solution.py:35
  106.8 21.8 %collective-permute-start.34 = (f32[768,128]{1,0:T(8,128)S(1)}, f32[768,128]{1,0:T(8,128)S(1)}, u32[]{:S(2)}, u32[]{:S(2)}) collective-permute-start(f32[768,128]{1,0:T(8,128)S(1)} %get-tuple-element.82), channel_id=1, source_target_pairs={{0,1},{1,0},{2,3},{3,2},{4,5},{5,4},{6,7},{7,6},{8,9},{9,8},{10,11... | collective-permute-start | bytes 1179656 | tf_op jit(solution)/shard_map/ppermute | solution.py:72
  114.0 14.7 %collective-permute-start.35 = (f32[768,128]{1,0:T(8,128)S(1)}, f32[768,128]{1,0:T(8,128)S(1)}, u32[]{:S(2)}, u32[]{:S(2)}) collective-permute-start(f32[768,128]{1,0:T(8,128)S(1)} %get-tuple-element.83), channel_id=1, source_target_pairs={{1,2},{2,1},{3,4},{4,3},{5,6},{6,5},{7,8},{8,7},{9,10},{10,9},{11,... | collective-permute-start | bytes 1179656 | tf_op jit(solution)/shard_map/ppermute | solution.py:71
  115.6 6.1 %collective-permute-start.29 = (f32[136,128]{1,0:T(8,128)S(1)}, f32[136,128]{1,0:T(8,128)S(1)}, u32[]{:S(2)}, u32[]{:S(2)}) collective-permute-start(f32[136,128]{1,0:T(8,128)S(1)} %add_add_fusion.3), channel_id=1, source_target_pairs={{0,16},{1,17},{2,18},{3,19},{4,20},{5,21},{6,22},{7,23},{8,24},{9,... | collective-permute-start | bytes 208904 | tf_op jit(solution)/shard_map/ppermute | solution.py:35
  117.1 9.2 %collective-permute-start.28 = (f32[136,128]{1,0:T(8,128)S(1)}, f32[136,128]{1,0:T(8,128)S(1)}, u32[]{:S(2)}, u32[]{:S(2)}) collective-permute-start(f32[136,128]{1,0:T(8,128)S(1)} %add_add_fusion.3), channel_id=1, source_target_pairs={{0,8},{1,9},{2,10},{3,11},{4,12},{5,13},{6,14},{7,15},{8,0},{9,1},... | collective-permute-start | bytes 208904 | tf_op jit(solution)/shard_map/ppermute | solution.py:35
  129.9 11.4 %collective-permute-start.40 = (f32[768,128]{1,0:T(8,128)S(1)}, f32[768,128]{1,0:T(8,128)S(1)}, u32[]{:S(2)}, u32[]{:S(2)}) collective-permute-start(f32[768,128]{1,0:T(8,128)S(1)} %get-tuple-element.87), channel_id=1, source_target_pairs={{0,1},{1,0},{2,3},{3,2},{4,5},{5,4},{6,7},{7,6},{8,9},{9,8},{10,11... | collective-permute-start | bytes 1179656 | tf_op jit(solution)/shard_map/ppermute | solution.py:72
  130.1 11.2 %collective-permute-start.41 = (f32[768,128]{1,0:T(8,128)S(1)}, f32[768,128]{1,0:T(8,128)S(1)}, u32[]{:S(2)}, u32[]{:S(2)}) collective-permute-start(f32[768,128]{1,0:T(8,128)S(1)} %get-tuple-element.88), channel_id=1, source_target_pairs={{1,2},{2,1},{3,4},{4,3},{5,6},{6,5},{7,8},{8,7},{9,10},{10,9},{11,... | collective-permute-start | bytes 1179656 | tf_op jit(solution)/shard_map/ppermute | solution.py:71
  136.9 17.2 %collective-permute-start.39 = (f32[136,128]{1,0:T(8,128)S(1)}, f32[136,128]{1,0:T(8,128)S(1)}, u32[]{:S(2)}, u32[]{:S(2)}) collective-permute-start(f32[136,128]{1,0:T(8,128)S(1)} %add.128), channel_id=1, source_target_pairs={{0,6},{1,7},{2,4},{3,5},{4,2},{5,3},{6,0},{7,1},{8,14},{9,15},{10,... | collective-permute-start | bytes 208904 | tf_op jit(solution)/shard_map/ppermute | solution.py:35
  139.5 17.8 %collective-permute-start.38 = (f32[136,128]{1,0:T(8,128)S(1)}, f32[136,128]{1,0:T(8,128)S(1)}, u32[]{:S(2)}, u32[]{:S(2)}) collective-permute-start(f32[136,128]{1,0:T(8,128)S(1)} %add.128), channel_id=1, source_target_pairs={{0,4},{1,5},{2,6},{3,7},{4,0},{5,1},{6,2},{7,3},{8,12},{9,13},{10,... | collective-permute-start | bytes 208904 | tf_op jit(solution)/shard_map/ppermute | solution.py:35
  140.4 16.9 %collective-permute-start.37 = (f32[136,128]{1,0:T(8,128)S(1)}, f32[136,128]{1,0:T(8,128)S(1)}, u32[]{:S(2)}, u32[]{:S(2)}) collective-permute-start(f32[136,128]{1,0:T(8,128)S(1)} %add.128), channel_id=1, source_target_pairs={{0,2},{1,3},{2,0},{3,1},{4,6},{5,7},{6,4},{7,5},{8,10},{9,11},{10,... | collective-permute-start | bytes 208904 | tf_op jit(solution)/shard_map/ppermute | solution.py:35
  (22 other events, 134.4 us)
